TPU v7x, 32 devices: a whole 2x2x4 slice. The times are simulated.
32 devices in a mesh: section: 4 (over y, x), dev: 8 (over z, core).
Axes of the slice: x: 2, y: 2, z: 4, core: 2. Of those that a mesh axis runs over, the one named last changes fastest.
Arguments:
- late_sent: bfloat16 [4, 784, 1024], P('section', 'dev'), may hold values from -5 to 5
- entry_rows: bfloat16 [784, 1024], P('dev'), may hold values from -5 to 5
- gain_first: float32 [4, 1024], P('section'), may hold values from 0.1 to 1.9
- shift_first: float32 [4, 1024], P('section'), may hold values from -3 to 3
- expand_late: bfloat16 [4, 1024, 4096], P('section', None, 'dev'), may hold values from -0.1875 to 0.1875
- gain_inner: float32 [4, 4096], P('section', 'dev'), may hold values from 0.1 to 1.9
- shift_inner: float32 [4, 4096], P('section', 'dev'), may hold values from -3 to 3
- reduce_late: bfloat16 [4, 4096, 1024], P('section', 'dev'), may hold values from -0.09375 to 0.09375
- early_saved: bfloat16 [4, 12544, 256], P('section', 'dev'), may hold values from -6 to 6
- upstream_grad: bfloat16 [4, 12544, 256], P('section', 'dev'), may hold values from -6 to 6
- exit_grad: bfloat16 [12544, 256], P('dev'), may hold values from -6 to 6
- expand_early: bfloat16 [4, 256, 1024], P('section'), may hold values from -0.375 to 0.375
- reduce_early: bfloat16 [4, 1024, 256], P('section'), may hold values from -0.1875 to 0.1875
Outputs:
- late_out: bfloat16 [4, 784, 1024], P('section', 'dev')
- input_grad: bfloat16 [4, 12544, 256], P('section', 'dev')
- grad_expand: float32 [4, 256, 1024], P('section')
- grad_reduce: float32 [4, 1024, 256], P('section')
All inputs are finite; a program needn't handle non-finite values.
Results may differ from a plain program's by a relative error of at most 0.02.
Values may be sent and summed in bfloat16 or wider, within the bound.
A program may use at most 128 MiB of HBM per device.

v0:
```python
import functools
import math

import jax
import jax.numpy as jnp
from jax import lax
from jax.experimental import pallas as pl
from jax.experimental.pallas import tpu as pltpu
from jax.sharding import PartitionSpec as P

MESH = pl.DeviceIdType.MESH
epsilon = 1e-05
H = 4
F32 = jnp.float32
BF16 = jnp.bfloat16


def sigmoid(x):
    return 0.5 * jnp.tanh(0.5 * x) + 0.5


def affine(sums, squares, count, gain, shift):
    average = sums / count
    second = squares / count
    spread = gain * lax.rsqrt(second - average * average + epsilon)
    return spread, shift - average * spread


def dot(a, b, ca=1, cb=0):
    return lax.dot_general(a, b, (((ca,), (cb,)), ((), ())), preferred_element_type=F32)


def kernel(
    sections, n_dev, chunk,
    late_hbm, entry_hbm, gain1, shift1, wexp_hbm, gain2, shift2, wred_hbm,
    saved_hbm, up_hbm, exit_hbm, eexp_hbm, ered_hbm,
    late_out, input_grad, gexp_out, gred_out,
    lbuf, first, hidden, part, prx, ltx, lrx,
    wexp, wred, saved, grad, eexp, ered, act, dsl, slope,
    gsum, gtx, gprx, wtx, wrx, abuf, turn,
    loc_sem, perm_send, perm_recv, gp_send, gp_recv,
    ag_s, ag_r, agp_s, agp_r, px_s, px_r, rs_s, rs_r,
    gx_s, gx_r, wrs_s, wrs_r, wag_s, wag_r, wagp_s, wagp_r,
):
    Q = n_dev // 2
    s = lax.axis_index("section")
    d = lax.axis_index("dev")
    q = d // 2
    c = lax.rem(d, 2)
    other = 1 - c
    partner = q * 2 + other
    rows = late_hbm.shape[0]
    half = late_hbm.shape[1] // H
    padded = first.shape[0] // n_dev
    e_rows = saved_hbm.shape[0]
    steps = e_rows // chunk
    total_rows = rows * n_dev
    hid = wexp.shape[1]

    def at_chip(offset):
        return lax.rem(q + offset + 2 * Q, Q)

    sgn = (1, -1) * (H // 2)
    nxt = tuple(at_chip(g) * 2 + c for g in sgn)

    barrier = pltpu.get_barrier_semaphore()
    for dev in (nxt[0], nxt[1], partner):
        pl.semaphore_signal(barrier, inc=1, device_id=(s, dev), device_id_type=MESH)

    @pl.when(s > 0)
    def _():
        pl.semaphore_signal(barrier, inc=1, device_id=(s - 1, d), device_id_type=MESH)

    @pl.when(s < sections - 1)
    def _():
        pl.semaphore_signal(barrier, inc=1, device_id=(s + 1, d), device_id_type=MESH)

    local = [
        pltpu.make_async_copy(src, dst, loc_sem.at[i])
        for i, (src, dst) in enumerate(
            ((saved_hbm, saved), (eexp_hbm, eexp), (ered_hbm, ered), (wexp_hbm, wexp), (wred_hbm, wred))
        )
    ]
    for copy in local:
        copy.start()

    pl.semaphore_wait(barrier, 3 + jnp.minimum(s, 1) + jnp.minimum(sections - 1 - s, 1))

    def remote(src, dst, send, recv, section, dev):
        return pltpu.make_async_remote_copy(
            src_ref=src, dst_ref=dst, send_sem=send, recv_sem=recv,
            device_id=(section, dev), device_id_type=MESH,
        )

    def cols(h):
        return pl.ds(h * half, half)

    def late_copy(h):
        return remote(
            late_hbm.at[:, cols(h)], lbuf.at[h, d], perm_send.at[h], perm_recv.at[h],
            jnp.minimum(s + 1, sections - 1), d,
        )

    def entry_copy(h):
        return pltpu.make_async_copy(entry_hbm.at[:, cols(h)], lbuf.at[h, d], perm_recv.at[h])

    def chunk_rows(j):
        return pl.ds(j * chunk, chunk)

    def grad_copy(j):
        return remote(
            up_hbm.at[chunk_rows(j)], grad.at[chunk_rows(j)], gp_send.at[j], gp_recv.at[j],
            jnp.maximum(s - 1, 0), d,
        )

    def exit_copy(j):
        return pltpu.make_async_copy(exit_hbm.at[chunk_rows(j)], grad.at[chunk_rows(j)], gp_recv.at[j])

    @pl.when(s < sections - 1)
    def _():
        for h in range(H):
            late_copy(h).start()

    @pl.when(s == 0)
    def _():
        for h in range(H):
            entry_copy(h).start()

    @pl.when(s > 0)
    def _():
        for j in range(steps):
            grad_copy(j).start()

    @pl.when(s == sections - 1)
    def _():
        for j in range(steps):
            exit_copy(j).start()

    def ring_gather(buf, ss, rr, ps, pr):
        def owner(h, t, lane):
            return at_chip(-sgn[h] * t) * 2 + lane

        def hop(h, t):
            piece = buf.at[h, owner(h, t, c)]
            return remote(piece, piece, ss.at[h, t], rr.at[h, t], s, nxt[h])

        def arrival(h, t):
            piece = buf.at[h, owner(h, t + 1, c)]
            return remote(piece, piece, ss.at[h, t], rr.at[h, t], s, nxt[h])

        def share(h, t, lane):
            piece = buf.at[h, owner(h, t, lane)]
            return remote(piece, piece, ps.at[h, t], pr.at[h, t], s, partner)

        def start(h):
            hop(h, 0).start()
            share(h, 0, c).start()

        def advance(h, t):
            arrival(h, t).wait_recv()
            if t + 1 < Q - 1:
                hop(h, t + 1).start()
            share(h, t + 1, c).start()

        def finish():
            for h in range(H):
                for t in range(Q):
                    share(h, t, other).wait_recv()

        def drain():
            for h in range(H):
                for t in range(Q - 1):
                    hop(h, t).wait_send()
                for t in range(Q):
                    share(h, t, c).wait_send()

        return start, advance, finish, drain

    def ring_scatter(mine, tx, rx, ss, rr):
        def hop(h, t):
            return remote(tx.at[h, t], rx.at[h, t], ss.at[h, t], rr.at[h, t], s, nxt[h])

        def start(h):
            tx[h, 0] = mine(h, at_chip(-sgn[h])).astype(BF16)
            hop(h, 0).start()

        def advance(h, t):
            hop(h, t).wait_recv()
            value = mine(h, at_chip(-sgn[h] * (t + 2))) + rx[h, t].astype(F32)
            if t == Q - 2:
                return value
            tx[h, t + 1] = value.astype(BF16)
            hop(h, t + 1).start()

        def drain():
            for h in range(H):
                for t in range(Q - 1):
                    hop(h, t).wait_send()

        return start, advance, drain

    def forward(j):
        at = chunk_rows(j)
        pre = dot(saved[at], eexp[...])
        sigma = sigmoid(pre)
        value = pre * sigma
        act[at] = value.astype(BF16)
        dsl[at] = sigma * (1.0 + pre - value)

    def backward(j):
        at = chunk_rows(j)

        @pl.when(s < sections - 1)
        def _():
            grad_copy(j).wait_recv()

        @pl.when(s == sections - 1)
        def _():
            exit_copy(j).wait()

        g = grad[at]
        back = dot(g, ered[...], 1, 1)
        sl = (back * dsl[at]).astype(BF16)
        slope[at] = sl
        input_grad[at] = (g.astype(F32) + dot(sl, eexp[...], 1, 1)).astype(BF16)

    local[0].wait()
    local[1].wait()
    fwd = 0
    first_part = max(steps // 2, 1)
    for j in range(first_part):
        forward(j)
    fwd = first_part

    @pl.when(s == 0)
    def _():
        for h in range(H):
            entry_copy(h).wait()

    @pl.when(s > 0)
    def _():
        for h in range(H):
            late_copy(h).wait_recv()

    ag_start, ag_advance, ag_finish, ag_drain = ring_gather(lbuf, ag_s, ag_r, agp_s, agp_r)
    for h in range(H):
        ag_start(h)
    for dev in range(n_dev):
        first[pl.ds((dev + 1) * padded - 16, 16), :] = jnp.zeros((16, first.shape[1]), BF16)
    for t in range(Q - 1):
        if fwd < steps:
            forward(fwd)
            fwd += 1
        if t == Q - 2:
            for j in range(fwd, steps):
                forward(j)
            fwd = steps
            local[2].wait()
            for j in range(steps // 2):
                backward(j)
        for h in range(H):
            ag_advance(h, t)

    for j in range(steps // 2, steps):
        backward(j)
    depth = gsum.shape[2]
    wide = eexp.shape[1]
    for n in range(wide // 256):
        at = pl.ds(n * 256, 256)
        gsum[0, :, :, at] = dot(saved[...], slope[:, at], 0, 0).reshape(Q, depth, 256)
        gsum[1, :, :, at] = dot(grad[...], act[:, at], 0, 0).reshape(Q, depth, 256)
    gtx[...] = gsum[other].astype(BF16)
    gx = remote(gtx, gprx, gx_s, gx_r, s, partner)
    gx.start()
    ag_finish()

    for h in range(H):
        total = jnp.zeros((1, half), F32)
        squares = jnp.zeros((1, half), F32)
        for dev in range(n_dev):
            v = lbuf[h, dev].astype(F32)
            total += jnp.sum(v, axis=0, keepdims=True)
            squares += jnp.sum(v * v, axis=0, keepdims=True)
        spread, offset = affine(total, squares, total_rows, gain1[:, cols(h)], shift1[:, cols(h)])
        for dev in range(n_dev):
            v = lbuf[h, dev].astype(F32) * spread + offset
            first[pl.ds(dev * padded, rows), cols(h)] = (v * sigmoid(v)).astype(BF16)

    gx.wait_recv()
    whalf = wide // H

    def wcols(h):
        return pl.ds(h * whalf, whalf)

    def weight_term(h, k):
        return gsum[c, k, :, wcols(h)] + gprx[k, :, wcols(h)].astype(F32)

    ws_start, ws_advance, ws_drain = ring_scatter(weight_term, wtx, wrx, wrs_s, wrs_r)
    wg_start, wg_advance, wg_finish, wg_drain = ring_gather(abuf, wag_s, wag_r, wagp_s, wagp_r)
    factor = 1.0 / math.sqrt(e_rows * n_dev)

    def weight_step(t):
        for h in range(H):
            value = ws_advance(h, t)
            if t == Q - 2:
                abuf[h, d] = (value * factor).astype(BF16)
                wg_start(h)

    for h in range(H):
        ws_start(h)

    local[3].wait()
    local[4].wait()
    width = min(256, hid)
    for n in range(hid // width):
        at = pl.ds(n * width, width)
        inner = dot(first[...], wexp[:, at])
        spread, offset = affine(
            jnp.sum(inner, axis=0, keepdims=True),
            jnp.sum(inner * inner, axis=0, keepdims=True),
            total_rows, gain2[:, at], shift2[:, at],
        )
        v = inner * spread + offset
        hidden[:, at] = (v * sigmoid(v)).astype(BF16)

    def pair_copy(h):
        return remote(part.at[other, h], prx.at[h], px_s.at[h], px_r.at[h], s, partner)

    tile = min(256, half)
    for h in range(H):
        for n in range(half // tile):
            value = dot(hidden[...], wred[:, pl.ds(h * half + n * tile, tile)]).astype(BF16)
            for dev in range(n_dev):
                part[dev % 2, h, dev // 2, :, pl.ds(n * tile, tile)] = value[dev * padded:dev * padded + rows]
        pair_copy(h).start()

    weight_step(0)

    def late_term(h, k):
        return part[c, h, k].astype(F32) + prx[h, k].astype(F32)

    rs_start, rs_advance, rs_drain = ring_scatter(late_term, ltx, lrx, rs_s, rs_r)
    for h in range(H):
        pair_copy(h).wait_recv()
        rs_start(h)

    for t in range(1, Q - 1):
        weight_step(t)
    for t in range(Q - 1):
        for h in range(H):
            value = rs_advance(h, t)
            if t == Q - 2:
                late_out[:, cols(h)] = (lbuf[h, d].astype(F32) + value).astype(BF16)
        for h in range(H):
            wg_advance(h, t)
    wg_finish()
    for h in range(H):
        for k in range(Q):
            at = pl.ds(k * depth, depth)
            gexp_out[at, wcols(h)] = abuf[h, 2 * k]
            turn[at, wcols(h)] = abuf[h, 2 * k + 1].astype(F32)
    for n in range(wide // 256):
        at = pl.ds(n * 256, 256)
        gred_out[at, :] = turn[:, at].T.astype(BF16)

    @pl.when(s < sections - 1)
    def _():
        for h in range(H):
            late_copy(h).wait_send()

    @pl.when(s > 0)
    def _():
        for j in range(steps):
            grad_copy(j).wait_send()

    ag_drain()
    for h in range(H):
        pair_copy(h).wait_send()
    rs_drain()
    gx.wait_send()
    ws_drain()
    wg_drain()


def shards(
    sections, n_dev,
    late_sent, entry_rows, gain_first, shift_first, expand_late, gain_inner, shift_inner,
    reduce_late, early_saved, upstream_grad, exit_grad, expand_early, reduce_early,
):
    rows, cl = entry_rows.shape
    e_rows, ce = exit_grad.shape
    fe = expand_early.shape[2]
    hid = expand_late.shape[2]
    Q = n_dev // 2
    half = cl // H
    padded = -(-rows // 16) * 16
    chunk = max(k for k in range(16, 257, 16) if e_rows % k == 0)
    steps = e_rows // chunk
    depth = ce // Q
    any_spec = pl.BlockSpec(memory_space=pl.ANY)
    vm = pl.BlockSpec(memory_space=pltpu.VMEM)
    V = pltpu.VMEM
    dma = pltpu.SemaphoreType.DMA
    ring = [dma((H, Q - 1)), dma((H, Q - 1))]
    late_out, input_grad, gexp, gred = pl.pallas_call(
        functools.partial(kernel, sections, n_dev, chunk),
        out_shape=(
            jax.ShapeDtypeStruct((rows, cl), BF16),
            jax.ShapeDtypeStruct((e_rows, ce), BF16),
            jax.ShapeDtypeStruct((ce, fe), BF16),
            jax.ShapeDtypeStruct((fe, ce), BF16),
        ),
        in_specs=[any_spec, any_spec, vm, vm, any_spec, vm, vm] + [any_spec] * 6,
        out_specs=(vm, vm, vm, vm),
        scratch_shapes=[
            V((H, n_dev, rows, half), BF16),
            V((n_dev * padded, cl), BF16),
            V((n_dev * padded, hid), BF16),
            V((2, H, Q, rows, half), BF16),
            V((H, Q, rows, half), BF16),
            V((H, Q - 1, rows, half), BF16),
            V((H, Q - 1, rows, half), BF16),
            V((cl, hid), BF16),
            V((hid, cl), BF16),
            V((e_rows, ce), BF16),
            V((e_rows, ce), BF16),
            V((ce, fe), BF16),
            V((fe, ce), BF16),
            V((e_rows, fe), BF16),
            V((e_rows, fe), F32),
            V((e_rows, fe), BF16),
            V((2, Q, depth, fe), F32),
            V((Q, depth, fe), BF16),
            V((Q, depth, fe), BF16),
            V((H, Q - 1, depth, fe // H), BF16),
            V((H, Q - 1, depth, fe // H), BF16),
            V((H, n_dev, depth, fe // H), BF16),
            V((ce, fe), F32),
            dma((5,)), dma((H,)), dma((H,)), dma((steps,)), dma((steps,)),
            *ring, dma((H, Q)), dma((H, Q)), dma((H,)), dma((H,)), *ring,
            dma, dma, *ring, *ring, dma((H, Q)), dma((H, Q)),
        ],
        compiler_params=pltpu.CompilerParams(
            collective_id=0, has_side_effects=True, vmem_limit_bytes=60 * 1024 * 1024
        ),
        name="relay",
    )(
        late_sent[0], entry_rows, gain_first, shift_first, expand_late[0], gain_inner, shift_inner,
        reduce_late[0], early_saved[0], upstream_grad[0], exit_grad, expand_early[0], reduce_early[0],
    )
    return late_out[None], input_grad[None], gexp.astype(F32)[None], gred.astype(F32)[None]


def solution(mesh):
    sections, n_dev = mesh.shape["section"], mesh.shape["dev"]
    sd, dd = P("section", "dev", None), P("dev", None)
    rep, one = P("section", None, None), P("section", None)
    in_specs = (
        sd, dd, one, one, P("section", None, "dev"), P("section", "dev"), P("section", "dev"),
        sd, sd, sd, dd, rep, rep,
    )
    return jax.shard_map(
        functools.partial(shards, sections, n_dev), mesh=mesh, in_specs=in_specs,
        out_specs=(sd, sd, rep, rep), check_vma=False,
    )
```

profile of v0, /device:TPU:5, one launch (start us, length us, event | category | flops | bytes accessed | tf_op | source)
XLA Modules:
  0.0 79.5 jit_solution(10265721613554579580)
XLA Ops:
  0.6 74.0 %relay.1 = (bf16[98,1024]{1,0:T(8,128)(2,1)}, bf16[1568,256]{1,0:T(8,128)(2,1)}, bf16[256,1024]{1,0:T(8,128)(2,1)}, bf16[1024,256]{1,0:T(8,128)(2,1)}) custom-call(bf16[98,1024]{1,0:T(8,128)(2,1)} %bitcast.23, bf16[98,1024]{1,0:T(8,128)(2,1)} %entry_hbm.1, f32[1,1024]{1,0:T(1,128)} %gain1.1, f32[1,1024]{1,0:T(1,128)} %shift1.1, bf16[1024,512]{1,0:T(8,128)(2,1)} %bitcast.15, ...), custom_call_target="tpu_custom_call" | custom-call | tf_op jit(solution)/shard_map/relay/pallas_call | solution.py:405
  74.7 0.0 copy-start.1
  74.7 2.2 %bitcast_convert_fusion.1 = f32[1,256,1024]{2,1,0:T(8,128)} fusion(bf16[256,1024]{1,0:T(8,128)(2,1)} %get-tuple-element.10), kind=kLoop, calls=%fused_computation.1 | loop fusion | flops 262144 | bytes 1572864 | tf_op jit(solution)/shard_map/broadcast_in_dim | solution.py:451
  76.9 0.0 copy-done.1
  76.9 0.0 copy-start.2
  76.9 0.0 copy-start
  76.9 1.0 %bitcast_convert_fusion = f32[1,1024,256]{2,1,0:T(8,128)} fusion(bf16[1024,256]{1,0:T(8,128)(2,1)S(1)} %copy-done.1), kind=kLoop, calls=%fused_computation | loop fusion | flops 262144 | bytes 1572864 | tf_op jit(solution)/shard_map/broadcast_in_dim | solution.py:451
  77.9 0.0 copy-done.2
  77.9 0.7 copy.19
  78.6 0.0 copy-done
  78.6 0.9 %copy.20 = bf16[1,1568,256]{2,1,0:T(8,128)(2,1)} copy(bf16[1,1568,256]{2,1,0:T(8,128)(2,1)S(1)} %bitcast.19) | data formatting | bytes 1605632
Async XLA Ops:
  74.7 2.2 %copy-start.1 = (bf16[1024,256]{1,0:T(8,128)(2,1)S(1)}, bf16[1024,256]{1,0:T(8,128)(2,1)}, u32[]{:S(2)}) copy-start(bf16[1024,256]{1,0:T(8,128)(2,1)} %get-tuple-element.11) | copy-start | bytes 1572868
  76.9 1.1 %copy-start.2 = (bf16[98,1024]{1,0:T(8,128)(2,1)S(1)}, bf16[98,1024]{1,0:T(8,128)(2,1)}, u32[]{:S(2)}) copy-start(bf16[98,1024]{1,0:T(8,128)(2,1)} %get-tuple-element.8) | copy-start | bytes 602116
  76.9 1.7 %copy-start = (bf16[1568,256]{1,0:T(8,128)(2,1)S(1)}, bf16[1568,256]{1,0:T(8,128)(2,1)}, u32[]{:S(2)}) copy-start(bf16[1568,256]{1,0:T(8,128)(2,1)} %get-tuple-element.9) | copy-start | bytes 2408452
where the time goes:
time: 79.7 us; the launch traced here: 79.5 us
  Pallas kernels  74 us (93%)
  other arithmetic  3.23 us (4%)
  local copies, waits for them, and re-layouts  1.58 us (2%)
    pallas_call x1, Pallas kernels, shards(): pl.pallas_call(functools.partial(kernel, sections, n_dev, chunk), out_sha...  74 us
    broadcast_in_dim x1, other arithmetic, shards(): gexp.astype(F32)[None]  2.18 us

commit v1 on v0

v1 whole, which is shorter than its diff:
```python
import functools
import math

import jax
import jax.numpy as jnp
from jax import lax
from jax.experimental import pallas as pl
from jax.experimental.pallas import tpu as pltpu
from jax.sharding import PartitionSpec as P

MESH = pl.DeviceIdType.MESH
epsilon = 1e-05
H = 4
SKEW = 3
F32 = jnp.float32
BF16 = jnp.bfloat16


def sigmoid(x):
    return 0.5 * jnp.tanh(0.5 * x) + 0.5


def affine(sums, squares, count, gain, shift):
    average = sums / count
    second = squares / count
    spread = gain * lax.rsqrt(second - average * average + epsilon)
    return spread, shift - average * spread


def dot(a, b, ca=1, cb=0):
    return lax.dot_general(a, b, (((ca,), (cb,)), ((), ())), preferred_element_type=F32)


def both(a, b):
    return jnp.logical_and(a, b)


def kernel(
    sections, n_dev, chunk, split,
    late_hbm, entry_hbm, gain1, shift1, wexp_hbm, gain2, shift2, wred_hbm,
    saved_hbm, up_hbm, exit_hbm, eexp_hbm, ered_hbm,
    late_out, input_grad, gout,
    stage, lbuf, first, inner, hidden, part, prx, rx,
    wexp, wred, saved, grad, eexp, ered, act, dsl, slope,
    gsum, gtx, gprx, wtx, wrx,
    loc_sem, perm_send, perm_recv, gp_send, gp_recv,
    ag_s, ag_r, agp_s, agp_r, px_s, px_r, gx_s, gx_r, st_s, st_r, wp_s, wp_r,
):
    Q = n_dev // 2
    s = lax.axis_index("section")
    d = lax.axis_index("dev")
    q = d // 2
    c = lax.rem(d, 2)
    other = 1 - c
    partner = q * 2 + other
    rows = late_hbm.shape[0]
    half = late_hbm.shape[1] // H
    padded = first.shape[0] // n_dev
    e_rows = saved_hbm.shape[0]
    steps = e_rows // chunk
    total_rows = rows * n_dev
    hid = wexp.shape[1]
    wide = eexp.shape[1]
    pieces, depth = gsum.shape[1], gsum.shape[2]
    factor = 1.0 / math.sqrt(e_rows * n_dev)

    last = Q - 1
    right, left = jnp.minimum(q + 1, last), jnp.maximum(q - 1, 0)
    nxt = (right * 2 + c, left * 2 + c)
    has_next = (q < last, q > 0)
    has_prev = (q > 0, q < last)
    hops = (q, last - q)

    barrier = pltpu.get_barrier_semaphore()
    pl.semaphore_signal(barrier, inc=1, device_id=(s, partner), device_id_type=MESH)
    for way in range(2):
        @pl.when(has_next[way])
        def _():
            pl.semaphore_signal(barrier, inc=1, device_id=(s, nxt[way]), device_id_type=MESH)

    @pl.when(s > 0)
    def _():
        pl.semaphore_signal(barrier, inc=1, device_id=(s - 1, d), device_id_type=MESH)

    @pl.when(s < sections - 1)
    def _():
        pl.semaphore_signal(barrier, inc=1, device_id=(s + 1, d), device_id_type=MESH)

    stage_copy = pltpu.make_async_copy(late_hbm, stage, loc_sem.at[5])
    stage_copy.start()
    local = [
        pltpu.make_async_copy(src, dst, loc_sem.at[i])
        for i, (src, dst) in enumerate(
            ((saved_hbm, saved), (eexp_hbm, eexp), (ered_hbm, ered), (wexp_hbm, wexp), (wred_hbm, wred))
        )
    ]
    for copy in local:
        copy.start()

    def remote(src, dst, send, recv, section, dev):
        return pltpu.make_async_remote_copy(
            src_ref=src, dst_ref=dst, send_sem=send, recv_sem=recv,
            device_id=(section, dev), device_id_type=MESH,
        )

    def cols(h):
        return pl.ds(h * half, half)

    def late_copy(h):
        return remote(
            stage.at[:, cols(h)], lbuf.at[h, d], perm_send.at[h], perm_recv.at[h],
            jnp.minimum(s + 1, sections - 1), d,
        )

    def entry_copy(h):
        return pltpu.make_async_copy(entry_hbm.at[:, cols(h)], lbuf.at[h, d], perm_recv.at[h])

    def chunk_rows(j):
        return pl.ds(j * chunk, chunk)

    def grad_copy(j):
        return remote(
            up_hbm.at[chunk_rows(j)], grad.at[chunk_rows(j)], gp_send.at[j], gp_recv.at[j],
            jnp.maximum(s - 1, 0), d,
        )

    def exit_copy(j):
        return pltpu.make_async_copy(exit_hbm.at[chunk_rows(j)], grad.at[chunk_rows(j)], gp_recv.at[j])

    stage_copy.wait()
    pl.semaphore_wait(
        barrier,
        1 + jnp.minimum(q, 1) + jnp.minimum(last - q, 1) + jnp.minimum(s, 1) + jnp.minimum(sections - 1 - s, 1),
    )

    @pl.when(s < sections - 1)
    def _():
        for h in range(H):
            late_copy(h).start()

    @pl.when(s == 0)
    def _():
        for h in range(H):
            entry_copy(h).start()

    @pl.when(s > 0)
    def _():
        for j in range(steps):
            grad_copy(j).start()

    @pl.when(s == sections - 1)
    def _():
        for j in range(steps):
            exit_copy(j).start()

    def source(way, k):
        return jnp.maximum(q - k, 0) if way == 0 else jnp.minimum(q + k, last)

    def have(way, k):
        return hops[way] >= k

    def hop(way, k, h):
        piece = lbuf.at[h, source(way, k) * 2 + c]
        return remote(piece, piece, ag_s.at[way, k, h], ag_r.at[way, k, h], s, nxt[way])

    def arrival(way, k, h):
        piece = lbuf.at[h, source(way, k) * 2 + c]
        return remote(piece, piece, ag_s.at[way, k - 1, h], ag_r.at[way, k - 1, h], s, nxt[way])

    def share(way, k, h, lane):
        piece = lbuf.at[h, source(way, k) * 2 + lane]
        return remote(piece, piece, agp_s.at[way, k, h], agp_r.at[way, k, h], s, partner)

    def own(h):
        @pl.when(s == 0)
        def _():
            entry_copy(h).wait()

        @pl.when(s > 0)
        def _():
            late_copy(h).wait_recv()

        for way in range(2):
            @pl.when(has_next[way])
            def _():
                hop(way, 0, h).start()
        share(0, 0, h, c).start()

    def relay(k, h):
        for way in range(2):
            @pl.when(have(way, k))
            def _():
                arrival(way, k, h).wait_recv()
                if k < last:
                    @pl.when(has_next[way])
                    def _():
                        hop(way, k, h).start()
                share(way, k, h, c).start()

    def gathered(h):
        share(0, 0, h, other).wait_recv()
        for k in range(1, Q):
            for way in range(2):
                @pl.when(have(way, k))
                def _():
                    share(way, k, h, other).wait_recv()

    def gather_drain():
        for h in range(H):
            share(0, 0, h, c).wait_send()
            for way in range(2):
                @pl.when(has_next[way])
                def _():
                    hop(way, 0, h).wait_send()
                for k in range(1, Q):
                    @pl.when(have(way, k))
                    def _():
                        share(way, k, h, c).wait_send()
                        if k < last:
                            @pl.when(has_next[way])
                            def _():
                                hop(way, k, h).wait_send()

    def forward(j):
        at = chunk_rows(j)
        pre = dot(saved[at], eexp[...])
        sigma = sigmoid(pre)
        value = pre * sigma
        act[at] = value.astype(BF16)
        dsl[at] = (sigma * (1.0 + pre - value)).astype(BF16)

    def backward(j):
        at = chunk_rows(j)

        @pl.when(s < sections - 1)
        def _():
            grad_copy(j).wait_recv()

        @pl.when(s == sections - 1)
        def _():
            exit_copy(j).wait()

        g = grad[at]
        back = dot(g, ered[...], 1, 1)
        sl = (back * dsl[at].astype(F32)).astype(BF16)
        slope[at] = sl
        input_grad[at] = (g.astype(F32) + dot(sl, eexp[...], 1, 1)).astype(BF16)

    def weight_sums(lo, hi):
        at = pl.ds(lo * chunk, (hi - lo) * chunk)
        for n in range(wide // 256):
            col = pl.ds(n * 256, 256)
            for which, (a, b) in enumerate(((saved, slope), (grad, act))):
                value = dot(a[at], b[at, col], 0, 0).reshape(pieces, depth, 256)
                if lo > 0:
                    value += gsum[which, :, :, col]
                gsum[which, :, :, col] = value

    local[0].wait()
    local[1].wait()
    early = max(steps // 2, 1)
    for j in range(early):
        forward(j)
    for dev in range(n_dev):
        first[pl.ds((dev + 1) * padded - 16, 16), :] = jnp.zeros((16, first.shape[1]), BF16)
    for way in range(2):
        @pl.when(hops[way] == 0)
        def _():
            wrx[way] = jnp.zeros(wrx.shape[1:], BF16)
            rx[way] = jnp.zeros(rx.shape[1:], BF16)
    for h in range(H):
        own(h)
        if early + h < steps:
            forward(early + h)
    for j in range(early + H, steps):
        forward(j)
    local[2].wait()
    local[3].wait()
    local[4].wait()

    def activate(h):
        total = jnp.zeros((1, half), F32)
        squares = jnp.zeros((1, half), F32)
        for dev in range(n_dev):
            v = lbuf[h, dev].astype(F32)
            total += jnp.sum(v, axis=0, keepdims=True)
            squares += jnp.sum(v * v, axis=0, keepdims=True)
        spread, offset = affine(total, squares, total_rows, gain1[:, cols(h)], shift1[:, cols(h)])
        for dev in range(n_dev):
            v = lbuf[h, dev].astype(F32) * spread + offset
            first[pl.ds(dev * padded, rows), cols(h)] = (v * sigmoid(v)).astype(BF16)

    width = min(256, hid)

    def expand(h):
        for n in range(hid // width):
            at = pl.ds(n * width, width)
            if split:
                value = dot(first[:, cols(h)], wexp[cols(h), at])
                if h > 0:
                    value += inner[:, at]
                if h < H - 1:
                    inner[:, at] = value
            elif h == H - 1:
                value = dot(first[...], wexp[:, at])
            if h == H - 1:
                spread, offset = affine(
                    jnp.sum(value, axis=0, keepdims=True),
                    jnp.sum(value * value, axis=0, keepdims=True),
                    total_rows, gain2[:, at], shift2[:, at],
                )
                v = value * spread + offset
                hidden[:, at] = (v * sigmoid(v)).astype(BF16)

    early_back = min(2, steps)
    for k in range(1, Q):
        if k == last:
            for j in range(early_back):
                backward(j)
        for h in range(H):
            relay(k, h)
            if k == last:
                gathered(h)
                activate(h)
                expand(h)

    def pair_copy(h):
        return remote(part.at[other, h], prx.at[h], px_s.at[h], px_r.at[h], s, partner)

    tile = min(256, half)
    for h in range(H):
        for n in range(half // tile):
            value = dot(hidden[...], wred[:, pl.ds(h * half + n * tile, tile)]).astype(BF16)
            for dev in range(n_dev):
                part[dev % 2, h, dev // 2, :, pl.ds(n * tile, tile)] = value[dev * padded:dev * padded + rows]
        pair_copy(h).start()

    far = last * H

    def mine(h, chip):
        return part[c, h, chip].astype(F32) + prx[h, chip].astype(F32)

    def goal(way, m):
        return last - m if way == 0 else m

    def row_hop(way, r):
        m, h = r // H, lax.rem(r, H)
        to = goal(way, m)
        i = r + pieces * jnp.minimum(m, 1)
        return remote(part.at[c, h, to], rx.at[way, h, to], st_s.at[way, i], st_r.at[way, i], s, nxt[way])

    def row_start(way, r):
        m, h = r // H, lax.rem(r, H)
        to = goal(way, m)
        part[c, h, to] = mine(h, to).astype(BF16)
        row_hop(way, r).start()

    def row_relay(way, r):
        m, h = r // H, lax.rem(r, H)
        to = goal(way, m)

        @pl.when(last - m >= hops[way])
        def _():
            row_hop(way, r).wait_recv()

        @pl.when(last - m > hops[way])
        def _():
            part[c, h, to] = (mine(h, to) + rx[way, h, to].astype(F32)).astype(BF16)
            row_hop(way, r).start()

    def each(lo, hi, body):
        def step(i, carry):
            body(i)
            return carry
        lax.fori_loop(lo, hi, step, 0)

    for h in range(H):
        pair_copy(h).wait_recv()
        for way in range(2):
            @pl.when(hops[way] == 0)
            def _():
                row_start(way, h)

    for j in range(early_back, steps - 1):
        backward(j)
    weight_sums(0, steps - 1)
    backward(steps - 1)
    weight_sums(steps - 1, steps)

    def gx(i):
        return remote(gtx.at[i], gprx.at[i], gx_s.at[i], gx_r.at[i], s, partner)

    for i in range(pieces):
        gtx[i] = gsum[other, i].astype(BF16)
        gx(i).start()

    def term(i):
        return gsum[c, i] + gprx[i].astype(F32)

    def sum_hop(way, i):
        return remote(wtx.at[way, i], wrx.at[way, i], st_s.at[way, H + i], st_r.at[way, H + i], s, nxt[way])

    def sum_first(i):
        gx(i).wait_recv()
        for way in range(2):
            @pl.when(hops[way] == 0)
            def _():
                wtx[way, i] = term(i).astype(BF16)
                sum_hop(way, i).start()

    def sum_relay(way, i):
        sum_hop(way, i).wait_recv()

        @pl.when(has_next[way])
        def _():
            wtx[way, i] = (term(i) + wrx[way, i].astype(F32)).astype(BF16)
            sum_hop(way, i).start()

    def give(i, lane):
        return remote(gout.at[lane, i], gout.at[lane, i], wp_s.at[i], wp_r.at[i], s, partner)

    def sum_finish(i):
        value = term(i) + (wrx[0, i].astype(F32) + wrx[1, i].astype(F32))
        gout[c, i] = (value * factor).astype(BF16)
        give(i, c).start()

    each(0, pieces, sum_first)

    def rest(r):
        for way in range(2):
            @pl.when(hops[way] == 0)
            def _():
                row_start(way, r)

    each(H, far, rest)

    count = far + pieces
    farther = jnp.maximum(hops[0], hops[1])

    def slot(t):
        for way in range(2):
            i = t - SKEW * hops[way]
            live = hops[way] > 0

            @pl.when(both(live, both(i >= 0, i < H)))
            def _():
                row_relay(way, i)

            @pl.when(both(live, both(i >= H, i < H + pieces)))
            def _():
                sum_relay(way, i - H)

            @pl.when(both(live, both(i >= H + pieces, i < count)))
            def _():
                row_relay(way, i - pieces)

        i = t - SKEW * farther - H

        @pl.when(both(i >= 0, i < pieces))
        def _():
            sum_finish(i)

    each(SKEW, count + SKEW * last, slot)

    for h in range(H):
        value = mine(h, q) + rx[0, h, q].astype(F32) + rx[1, h, q].astype(F32)
        late_out[:, cols(h)] = (lbuf[h, d].astype(F32) + value).astype(BF16)

    @pl.when(s < sections - 1)
    def _():
        for h in range(H):
            late_copy(h).wait_send()

    @pl.when(s > 0)
    def _():
        for j in range(steps):
            grad_copy(j).wait_send()

    gather_drain()
    for h in range(H):
        pair_copy(h).wait_send()

    def drain_rows(r):
        for way in range(2):
            @pl.when(last - r // H > hops[way])
            def _():
                row_hop(way, r).wait_send()

    each(0, far, drain_rows)

    def drain_sums(i):
        gx(i).wait_send()
        give(i, c).wait_send()
        for way in range(2):
            @pl.when(has_next[way])
            def _():
                sum_hop(way, i).wait_send()

    each(0, pieces, drain_sums)
    for i in range(pieces):
        give(i, other).wait_recv()


def finish(late_in, grad_in, sums, late_out, input_grad, gexp, gred, wide_e, wide_r, sem):
    ce, fe = wide_e.shape
    a = pltpu.make_async_copy(grad_in, input_grad.at[0], sem.at[0])
    b = pltpu.make_async_copy(late_in, late_out.at[0], sem.at[1])
    a.start()
    b.start()
    wide_e[...] = sums[0].reshape(ce, fe).astype(F32)
    x = pltpu.make_async_copy(wide_e, gexp.at[0], sem.at[2])
    x.start()
    for n in range(fe // 256):
        at = pl.ds(n * 256, 256)
        wide_r[at, :] = sums[1, :, :, at].reshape(ce, 256).astype(F32).T
    y = pltpu.make_async_copy(wide_r, gred.at[0], sem.at[3])
    y.start()
    for copy in (a, b, x, y):
        copy.wait()


def shards(
    sections, n_dev,
    late_sent, entry_rows, gain_first, shift_first, expand_late, gain_inner, shift_inner,
    reduce_late, early_saved, upstream_grad, exit_grad, expand_early, reduce_early,
):
    rows, cl = entry_rows.shape
    e_rows, ce = exit_grad.shape
    fe = expand_early.shape[2]
    hid = expand_late.shape[2]
    Q = n_dev // 2
    half = cl // H
    padded = -(-rows // 16) * 16
    chunk = max(k for k in range(16, 257, 16) if e_rows % k == 0)
    steps = e_rows // chunk
    pieces = ce // 32
    depth = ce // pieces
    count = (Q - 1) * H + pieces
    split = n_dev * padded * hid * 4 <= 4 * 1024 * 1024
    hbm = pl.BlockSpec(memory_space=pltpu.HBM)
    any_spec = pl.BlockSpec(memory_space=pl.ANY)
    vm = pl.BlockSpec(memory_space=pltpu.VMEM)
    V = pltpu.VMEM
    dma = pltpu.SemaphoreType.DMA
    late_out, input_grad, sums = pl.pallas_call(
        functools.partial(kernel, sections, n_dev, chunk, split),
        out_shape=(
            V((rows, cl), BF16),
            V((e_rows, ce), BF16),
            V((2, pieces, depth, fe), BF16),
        ),
        in_specs=[hbm, hbm, vm, vm, hbm, vm, vm] + [hbm] * 6,
        out_specs=(vm, vm, vm),
        scratch_shapes=[
            V((rows, cl), BF16),
            V((H, n_dev, rows, half), BF16),
            V((n_dev * padded, cl), BF16),
            V((n_dev * padded, hid) if split else (8, 128), F32),
            V((n_dev * padded, hid), BF16),
            V((2, H, Q, rows, half), BF16),
            V((H, Q, rows, half), BF16),
            V((2, H, Q, rows, half), BF16),
            V((cl, hid), BF16),
            V((hid, cl), BF16),
            V((e_rows, ce), BF16),
            V((e_rows, ce), BF16),
            V((ce, fe), BF16),
            V((fe, ce), BF16),
            V((e_rows, fe), BF16),
            V((e_rows, fe), BF16),
            V((e_rows, fe), BF16),
            V((2, pieces, depth, fe), F32),
            V((pieces, depth, fe), BF16),
            V((pieces, depth, fe), BF16),
            V((2, pieces, depth, fe), BF16),
            V((2, pieces, depth, fe), BF16),
            dma((6,)), dma((H,)), dma((H,)), dma((steps,)), dma((steps,)),
            dma((2, Q - 1, H)), dma((2, Q - 1, H)), dma((2, Q, H)), dma((2, Q, H)),
            dma((H,)), dma((H,)), dma((pieces,)), dma((pieces,)),
            dma((2, count)), dma((2, count)), dma((pieces,)), dma((pieces,)),
        ],
        compiler_params=pltpu.CompilerParams(
            collective_id=0, has_side_effects=True, vmem_limit_bytes=60 * 1024 * 1024
        ),
        name="relay",
    )(
        late_sent[0], entry_rows, gain_first, shift_first, expand_late[0], gain_inner, shift_inner,
        reduce_late[0], early_saved[0], upstream_grad[0], exit_grad, expand_early[0], reduce_early[0],
    )
    return pl.pallas_call(
        finish,
        out_shape=(
            jax.ShapeDtypeStruct((1, rows, cl), BF16),
            jax.ShapeDtypeStruct((1, e_rows, ce), BF16),
            jax.ShapeDtypeStruct((1, ce, fe), F32),
            jax.ShapeDtypeStruct((1, fe, ce), F32),
        ),
        in_specs=[vm, vm, vm],
        out_specs=(any_spec,) * 4,
        scratch_shapes=[V((ce, fe), F32), V((fe, ce), F32), dma((4,))],
        compiler_params=pltpu.CompilerParams(vmem_limit_bytes=16 * 1024 * 1024),
        name="finish",
    )(late_out, input_grad, sums)


def solution(mesh):
    sections, n_dev = mesh.shape["section"], mesh.shape["dev"]
    sd, dd = P("section", "dev", None), P("dev", None)
    rep, one = P("section", None, None), P("section", None)
    in_specs = (
        sd, dd, one, one, P("section", None, "dev"), P("section", "dev"), P("section", "dev"),
        sd, sd, sd, dd, rep, rep,
    )
    return jax.shard_map(
        functools.partial(shards, sections, n_dev), mesh=mesh, in_specs=in_specs,
        out_specs=(sd, sd, rep, rep), check_vma=False,
    )
```

time: 79.7 us -> 64.4 us (0.81)
  Pallas kernels: 74 us -> 63.4 us
  other arithmetic: 3.23 us -> 0 us
  local copies, waits for them, and re-layouts: 1.58 us -> 0 us
    pallas_call x1 -> x2, Pallas kernels: 74 us -> 63.4 us  [the longest x1 61.7 us: shards(): pl.pallas_call(functools.partial(kernel, sections, n_dev, chunk, split),...]
    broadcast_in_dim x2 -> x0, other arithmetic: 3.23 us -> none  [the longest x1 2.18 us: shards(): gexp.astype(F32)[None]]
    unnamed x8 -> x0, local copies, waits for them, and re-layouts: 1.58 us -> none
where the time goes in v1:
time: 64.4 us; the launch traced here: 64.2 us
  Pallas kernels  63.4 us (98%)
  between operations  0.8 us (1%)
    pallas_call x1, Pallas kernels, shards(): pl.pallas_call(functools.partial(kernel, sections, n_dev, chunk, split),...  61.7 us
    pallas_call x1, Pallas kernels, shards(): pl.pallas_call(finish, out_shape=(jax.ShapeDtypeStruct((1, rows, cl), BF1...  1.69 us

profile of v1, /device:TPU:5, one launch (start us, length us, event | category | flops | bytes accessed | tf_op | source)
XLA Modules:
  0.0 64.2 jit_solution(12444702597602338300)
XLA Ops:
  0.6 61.7 %relay.1 = (bf16[98,1024]{1,0:T(8,128)(2,1)S(1)}, bf16[1568,256]{1,0:T(8,128)(2,1)S(1)}, bf16[2,8,32,1024]{3,2,1,0:T(8,128)(2,1)S(1)}) custom-call(bf16[98,1024]{1,0:T(8,128)(2,1)} %bitcast.13, bf16[98,1024]{1,0:T(8,128)(2,1)} %entry_hbm.1, f32[1,1024]{1,0:T(1,128)} %gain1.1, f32[1,1024]{1,0:T(1,128)} %shift1.1, bf16[1024,512]{1,0:T(8,128)(2,1)} %bitcast.7, ...), custom_call_target="tpu_custom_call" | custom-call | tf_op jit(solution)/shard_map/relay/pallas_call | solution.py:545
  62.4 1.7 %finish.1 = (bf16[1,98,1024]{2,1,0:T(8,128)(2,1)}, bf16[1,1568,256]{2,1,0:T(8,128)(2,1)}, f32[1,256,1024]{2,1,0:T(8,128)}, f32[1,1024,256]{2,1,0:T(8,128)}) custom-call(bf16[98,1024]{1,0:T(8,128)(2,1)S(1)} %get-tuple-element.7.late_in, bf16[1568,256]{1,0:T(8,128)(2,1)S(1)} %get-tuple-element.8.grad_in, bf16[2,8,32,1024]{3,2,1,0:T(8,128)(2,1)S(1)} %get-tuple-element.9.sums), custom_call_target="tpu_custom_call" | custom-call | tf_op jit(solution)/shard_map/finish/pallas_call | solution.py:590

commit v2 on v1

--- a/solution.py
+++ b/solution.py
@@ -16,8 +16,9 @@
 BF16 = jnp.bfloat16
 
 
-def sigmoid(x):
-    return 0.5 * jnp.tanh(0.5 * x) + 0.5
+def scaled_silu(x, spread, offset):
+    u = x * (0.5 * spread) + 0.5 * offset
+    return u * jnp.tanh(u) + u
 
 
 def affine(sums, squares, count, gain, shift):
@@ -224,8 +225,10 @@
     def forward(j):
         at = chunk_rows(j)
         pre = dot(saved[at], eexp[...])
-        sigma = sigmoid(pre)
-        value = pre * sigma
+        u = 0.5 * pre
+        bent = jnp.tanh(u)
+        sigma = 0.5 * bent + 0.5
+        value = u * bent + u
         act[at] = value.astype(BF16)
         dsl[at] = (sigma * (1.0 + pre - value)).astype(BF16)
 
@@ -240,21 +243,22 @@
         def _():
             exit_copy(j).wait()
 
-        g = grad[at]
-        back = dot(g, ered[...], 1, 1)
-        sl = (back * dsl[at].astype(F32)).astype(BF16)
-        slope[at] = sl
-        input_grad[at] = (g.astype(F32) + dot(sl, eexp[...], 1, 1)).astype(BF16)
-
-    def weight_sums(lo, hi):
+        back = dot(grad[at], ered[...], 1, 1)
+        slope[at] = (back * dsl[at].astype(F32)).astype(BF16)
+
+    def downward(j):
+        at = chunk_rows(j)
+        input_grad[at] = (grad[at].astype(F32) + dot(slope[at], eexp[...], 1, 1)).astype(BF16)
+
+    def weight_sums(which, lo, hi):
         at = pl.ds(lo * chunk, (hi - lo) * chunk)
+        a, b = ((saved, slope), (grad, act))[which]
         for n in range(wide // 256):
             col = pl.ds(n * 256, 256)
-            for which, (a, b) in enumerate(((saved, slope), (grad, act))):
-                value = dot(a[at], b[at, col], 0, 0).reshape(pieces, depth, 256)
-                if lo > 0:
-                    value += gsum[which, :, :, col]
-                gsum[which, :, :, col] = value
+            value = dot(a[at], b[at, col], 0, 0).reshape(pieces, depth, 256)
+            if lo > 0:
+                value += gsum[which, :, :, col]
+            gsum[which, :, :, col] = value
 
     local[0].wait()
     local[1].wait()
@@ -287,8 +291,8 @@
             squares += jnp.sum(v * v, axis=0, keepdims=True)
         spread, offset = affine(total, squares, total_rows, gain1[:, cols(h)], shift1[:, cols(h)])
         for dev in range(n_dev):
-            v = lbuf[h, dev].astype(F32) * spread + offset
-            first[pl.ds(dev * padded, rows), cols(h)] = (v * sigmoid(v)).astype(BF16)
+            v = scaled_silu(lbuf[h, dev].astype(F32), spread, offset)
+            first[pl.ds(dev * padded, rows), cols(h)] = v.astype(BF16)
 
     width = min(256, hid)
 
@@ -309,23 +313,79 @@
                     jnp.sum(value * value, axis=0, keepdims=True),
                     total_rows, gain2[:, at], shift2[:, at],
                 )
-                v = value * spread + offset
-                hidden[:, at] = (v * sigmoid(v)).astype(BF16)
-
-    early_back = min(2, steps)
-    for k in range(1, Q):
-        if k == last:
-            for j in range(early_back):
-                backward(j)
+                hidden[:, at] = scaled_silu(value, spread, offset).astype(BF16)
+
+    done = 0
+    ready = min(2, steps - 1)
+    for k in range(1, last):
         for h in range(H):
             relay(k, h)
-            if k == last:
-                gathered(h)
-                activate(h)
-                expand(h)
+            if k == last - 1 and h in (1, 2) and done < ready:
+                backward(done)
+                downward(done)
+                done += 1
+    weight_sums(0, 0, done)
+    for h in range(H):
+        relay(last, h)
+        if h == 0 and done < steps - 1:
+            backward(done)
+            done += 1
+        if h > 0:
+            gathered(h - 1)
+            activate(h - 1)
+            expand(h - 1)
+    gathered(H - 1)
+    activate(H - 1)
+    expand(H - 1)
 
     def pair_copy(h):
         return remote(part.at[other, h], prx.at[h], px_s.at[h], px_r.at[h], s, partner)
+
+    far = last * H
+
+    def mine(h, chip):
+        return part[c, h, chip].astype(F32) + prx[h, chip].astype(F32)
+
+    def goal(way, m):
+        return last - m if way == 0 else m
+
+    def row_hop(way, r):
+        m, h = r // H, lax.rem(r, H)
+        to = goal(way, m)
+        i = r + pieces * jnp.minimum(m, 1)
+        return remote(part.at[c, h, to], rx.at[way, h, to], st_s.at[way, i], st_r.at[way, i], s, nxt[way])
+
+    def row_start(way, r):
+        m, h = r // H, lax.rem(r, H)
+        to = goal(way, m)
+        part[c, h, to] = mine(h, to).astype(BF16)
+        row_hop(way, r).start()
+
+    def row_relay(way, r):
+        m, h = r // H, lax.rem(r, H)
+        to = goal(way, m)
+
+        @pl.when(last - m >= hops[way])
+        def _():
+            row_hop(way, r).wait_recv()
+
+        @pl.when(last - m > hops[way])
+        def _():
+            part[c, h, to] = (mine(h, to) + rx[way, h, to].astype(F32)).astype(BF16)
+            row_hop(way, r).start()
+
+    def each(lo, hi, body):
+        def step(i, carry):
+            body(i)
+            return carry
+        lax.fori_loop(lo, hi, step, 0)
+
+    def scatter(h):
+        pair_copy(h).wait_recv()
+        for way in range(2):
+            @pl.when(hops[way] == 0)
+            def _():
+                row_start(way, h)
 
     tile = min(256, half)
     for h in range(H):
@@ -334,65 +394,33 @@
             for dev in range(n_dev):
                 part[dev % 2, h, dev // 2, :, pl.ds(n * tile, tile)] = value[dev * padded:dev * padded + rows]
         pair_copy(h).start()
-
-    far = last * H
-
-    def mine(h, chip):
-        return part[c, h, chip].astype(F32) + prx[h, chip].astype(F32)
-
-    def goal(way, m):
-        return last - m if way == 0 else m
-
-    def row_hop(way, r):
-        m, h = r // H, lax.rem(r, H)
-        to = goal(way, m)
-        i = r + pieces * jnp.minimum(m, 1)
-        return remote(part.at[c, h, to], rx.at[way, h, to], st_s.at[way, i], st_r.at[way, i], s, nxt[way])
-
-    def row_start(way, r):
-        m, h = r // H, lax.rem(r, H)
-        to = goal(way, m)
-        part[c, h, to] = mine(h, to).astype(BF16)
-        row_hop(way, r).start()
-
-    def row_relay(way, r):
-        m, h = r // H, lax.rem(r, H)
-        to = goal(way, m)
-
-        @pl.when(last - m >= hops[way])
-        def _():
-            row_hop(way, r).wait_recv()
-
-        @pl.when(last - m > hops[way])
-        def _():
-            part[c, h, to] = (mine(h, to) + rx[way, h, to].astype(F32)).astype(BF16)
-            row_hop(way, r).start()
-
-    def each(lo, hi, body):
-        def step(i, carry):
-            body(i)
-            return carry
-        lax.fori_loop(lo, hi, step, 0)
-
-    for h in range(H):
-        pair_copy(h).wait_recv()
-        for way in range(2):
-            @pl.when(hops[way] == 0)
-            def _():
-                row_start(way, h)
-
-    for j in range(early_back, steps - 1):
-        backward(j)
-    weight_sums(0, steps - 1)
-    backward(steps - 1)
-    weight_sums(steps - 1, steps)
+        if h > 0:
+            scatter(h - 1)
 
     def gx(i):
         return remote(gtx.at[i], gprx.at[i], gx_s.at[i], gx_r.at[i], s, partner)
 
-    for i in range(pieces):
-        gtx[i] = gsum[other, i].astype(BF16)
-        gx(i).start()
+    def exchange(which):
+        @pl.when(other == which)
+        def _():
+            for i in range(pieces):
+                gtx[i] = gsum[which, i].astype(BF16)
+                gx(i).start()
+
+    counted = ready
+    backward(done)
+    scatter(H - 1)
+    for j in range(done + 1, steps):
+        backward(j)
+    weight_sums(1, 0, steps)
+    exchange(1)
+    weight_sums(0, counted, steps)
+    exchange(0)
+    for h in range(H):
+        for way in range(2):
+            @pl.when(hops[way] == 1)
+            def _():
+                row_relay(way, h)
 
     def term(i):
         return gsum[c, i] + gprx[i].astype(F32)
@@ -433,6 +461,8 @@
                 row_start(way, r)
 
     each(H, far, rest)
+    for j in range(counted, steps):
+        downward(j)
 
     count = far + pieces
     farther = jnp.maximum(hops[0], hops[1])
@@ -442,7 +472,7 @@
             i = t - SKEW * hops[way]
             live = hops[way] > 0
 
-            @pl.when(both(live, both(i >= 0, i < H)))
+            @pl.when(both(hops[way] > 1, both(i >= 0, i < H)))
             def _():
                 row_relay(way, i)
 
@@ -459,26 +489,26 @@
         @pl.when(both(i >= 0, i < pieces))
         def _():
             sum_finish(i)
+
+    @pl.when(s < sections - 1)
+    def _():
+        for h in range(H):
+            late_copy(h).wait_send()
+
+    @pl.when(s > 0)
+    def _():
+        for j in range(steps):
+            grad_copy(j).wait_send()
+
+    gather_drain()
+    for h in range(H):
+        pair_copy(h).wait_send()
 
     each(SKEW, count + SKEW * last, slot)
 
     for h in range(H):
         value = mine(h, q) + rx[0, h, q].astype(F32) + rx[1, h, q].astype(F32)
         late_out[:, cols(h)] = (lbuf[h, d].astype(F32) + value).astype(BF16)
-
-    @pl.when(s < sections - 1)
-    def _():
-        for h in range(H):
-            late_copy(h).wait_send()
-
-    @pl.when(s > 0)
-    def _():
-        for j in range(steps):
-            grad_copy(j).wait_send()
-
-    gather_drain()
-    for h in range(H):
-        pair_copy(h).wait_send()
 
     def drain_rows(r):
         for way in range(2):

time: 64.4 us -> 59.8 us (0.929)
  Pallas kernels: 63.4 us -> 58.9 us
    pallas_call x1, Pallas kernels: 61.7 us -> 57.2 us  [shards(): pl.pallas_call(functools.partial(kernel, sections, n_dev, chunk, split),...]
where the time goes in v2:
time: 59.8 us; the launch traced here: 59.6 us
  Pallas kernels  58.9 us (98%)
  between operations  0.64 us (1%)
    pallas_call x1, Pallas kernels, shards(): pl.pallas_call(functools.partial(kernel, sections, n_dev, chunk, split),...  57.2 us
    pallas_call x1, Pallas kernels, shards(): pl.pallas_call(finish, out_shape=(jax.ShapeDtypeStruct((1, rows, cl), BF1...  1.69 us

profile of v2, /device:TPU:5, one launch (start us, length us, event | category | flops | bytes accessed | tf_op | source)
XLA Modules:
  0.0 59.6 jit_solution(2007811899379878494)
XLA Ops:
  0.6 57.2 %relay.1 = (bf16[98,1024]{1,0:T(8,128)(2,1)S(1)}, bf16[1568,256]{1,0:T(8,128)(2,1)S(1)}, bf16[2,8,32,1024]{3,2,1,0:T(8,128)(2,1)S(1)}) custom-call(bf16[98,1024]{1,0:T(8,128)(2,1)} %bitcast.13, bf16[98,1024]{1,0:T(8,128)(2,1)} %entry_hbm.1, f32[1,1024]{1,0:T(1,128)} %gain1.1, f32[1,1024]{1,0:T(1,128)} %shift1.1, bf16[1024,512]{1,0:T(8,128)(2,1)} %bitcast.7, ...), custom_call_target="tpu_custom_call" | custom-call | tf_op jit(solution)/shard_map/relay/pallas_call | solution.py:575
  57.9 1.7 %finish.1 = (bf16[1,98,1024]{2,1,0:T(8,128)(2,1)}, bf16[1,1568,256]{2,1,0:T(8,128)(2,1)}, f32[1,256,1024]{2,1,0:T(8,128)}, f32[1,1024,256]{2,1,0:T(8,128)}) custom-call(bf16[98,1024]{1,0:T(8,128)(2,1)S(1)} %get-tuple-element.7.late_in, bf16[1568,256]{1,0:T(8,128)(2,1)S(1)} %get-tuple-element.8.grad_in, bf16[2,8,32,1024]{3,2,1,0:T(8,128)(2,1)S(1)} %get-tuple-element.9.sums), custom_call_target="tpu_custom_call" | custom-call | tf_op jit(solution)/shard_map/finish/pallas_call | solution.py:620

commit v3 on v2

--- a/solution.py
+++ b/solution.py
@@ -12,6 +12,7 @@
 epsilon = 1e-05
 H = 4
 SKEW = 3
+LEAD = 2
 F32 = jnp.float32
 BF16 = jnp.bfloat16
 
@@ -63,6 +64,9 @@
     hid = wexp.shape[1]
     wide = eexp.shape[1]
     pieces, depth = gsum.shape[1], gsum.shape[2]
+    ce = grad.shape[1]
+    front = pieces // 2
+    ahead = front * depth
     factor = 1.0 / math.sqrt(e_rows * n_dev)
 
     last = Q - 1
@@ -119,14 +123,28 @@
     def chunk_rows(j):
         return pl.ds(j * chunk, chunk)
 
+    def grad_at(j):
+        if j == steps:
+            return slice(None), pl.ds(0, ahead)
+        return chunk_rows(j), pl.ds(ahead, ce - ahead)
+
     def grad_copy(j):
         return remote(
-            up_hbm.at[chunk_rows(j)], grad.at[chunk_rows(j)], gp_send.at[j], gp_recv.at[j],
+            up_hbm.at[grad_at(j)], grad.at[grad_at(j)], gp_send.at[j], gp_recv.at[j],
             jnp.maximum(s - 1, 0), d,
         )
 
     def exit_copy(j):
-        return pltpu.make_async_copy(exit_hbm.at[chunk_rows(j)], grad.at[chunk_rows(j)], gp_recv.at[j])
+        return pltpu.make_async_copy(exit_hbm.at[grad_at(j)], grad.at[grad_at(j)], gp_recv.at[j])
+
+    def grad_wait(j):
+        @pl.when(s < sections - 1)
+        def _():
+            grad_copy(j).wait_recv()
+
+        @pl.when(s == sections - 1)
+        def _():
+            exit_copy(j).wait()
 
     stage_copy.wait()
     pl.semaphore_wait(
@@ -146,12 +164,12 @@
 
     @pl.when(s > 0)
     def _():
-        for j in range(steps):
+        for j in (steps, *range(steps)):
             grad_copy(j).start()
 
     @pl.when(s == sections - 1)
     def _():
-        for j in range(steps):
+        for j in (steps, *range(steps)):
             exit_copy(j).start()
 
     def source(way, k):
@@ -234,15 +252,7 @@
 
     def backward(j):
         at = chunk_rows(j)
-
-        @pl.when(s < sections - 1)
-        def _():
-            grad_copy(j).wait_recv()
-
-        @pl.when(s == sections - 1)
-        def _():
-            exit_copy(j).wait()
-
+        grad_wait(j)
         back = dot(grad[at], ered[...], 1, 1)
         slope[at] = (back * dsl[at].astype(F32)).astype(BF16)
 
@@ -251,14 +261,11 @@
         input_grad[at] = (grad[at].astype(F32) + dot(slope[at], eexp[...], 1, 1)).astype(BF16)
 
     def weight_sums(which, lo, hi):
-        at = pl.ds(lo * chunk, (hi - lo) * chunk)
         a, b = ((saved, slope), (grad, act))[which]
+        at = pl.ds(lo * depth, (hi - lo) * depth)
         for n in range(wide // 256):
             col = pl.ds(n * 256, 256)
-            value = dot(a[at], b[at, col], 0, 0).reshape(pieces, depth, 256)
-            if lo > 0:
-                value += gsum[which, :, :, col]
-            gsum[which, :, :, col] = value
+            gsum[which, lo:hi, :, col] = dot(a[:, at], b[:, col], 0, 0).reshape(hi - lo, depth, 256)
 
     local[0].wait()
     local[1].wait()
@@ -315,21 +322,56 @@
                 )
                 hidden[:, at] = scaled_silu(value, spread, offset).astype(BF16)
 
-    done = 0
-    ready = min(2, steps - 1)
+    def gx(i):
+        return remote(gtx.at[i], gprx.at[i], gx_s.at[i], gx_r.at[i], s, partner)
+
+    def exchange(which, lo, hi):
+        @pl.when(other == which)
+        def _():
+            for i in range(lo, hi):
+                gtx[i] = gsum[which, i].astype(BF16)
+                gx(i).start()
+
+    def term(i):
+        return gsum[c, i] + gprx[i].astype(F32)
+
+    def sum_hop(way, i):
+        at = far + i
+        return remote(wtx.at[way, i], wrx.at[way, i], st_s.at[way, at], st_r.at[way, at], s, nxt[way])
+
+    def sum_first(i):
+        gx(i).wait_recv()
+        for way in range(2):
+            @pl.when(hops[way] == 0)
+            def _():
+                wtx[way, i] = term(i).astype(BF16)
+                sum_hop(way, i).start()
+
+    def sum_relay(way, i):
+        sum_hop(way, i).wait_recv()
+
+        @pl.when(has_next[way])
+        def _():
+            wtx[way, i] = (term(i) + wrx[way, i].astype(F32)).astype(BF16)
+            sum_hop(way, i).start()
+
+    def each(lo, hi, body):
+        def step(i, carry):
+            body(i)
+            return carry
+        lax.fori_loop(lo, hi, step, 0)
+
+    far = last * H
+    lead = min(H + LEAD, far)
     for k in range(1, last):
         for h in range(H):
             relay(k, h)
-            if k == last - 1 and h in (1, 2) and done < ready:
-                backward(done)
-                downward(done)
-                done += 1
-    weight_sums(0, 0, done)
     for h in range(H):
         relay(last, h)
-        if h == 0 and done < steps - 1:
-            backward(done)
-            done += 1
+        if h == H - 1:
+            grad_wait(steps)
+            weight_sums(1, 0, front)
+            exchange(1, 0, front)
         if h > 0:
             gathered(h - 1)
             activate(h - 1)
@@ -338,10 +380,12 @@
     activate(H - 1)
     expand(H - 1)
 
+    @pl.when(c == 1)
+    def _():
+        each(0, front, sum_first)
+
     def pair_copy(h):
         return remote(part.at[other, h], prx.at[h], px_s.at[h], px_r.at[h], s, partner)
-
-    far = last * H
 
     def mine(h, chip):
         return part[c, h, chip].astype(F32) + prx[h, chip].astype(F32)
@@ -352,8 +396,7 @@
     def row_hop(way, r):
         m, h = r // H, lax.rem(r, H)
         to = goal(way, m)
-        i = r + pieces * jnp.minimum(m, 1)
-        return remote(part.at[c, h, to], rx.at[way, h, to], st_s.at[way, i], st_r.at[way, i], s, nxt[way])
+        return remote(part.at[c, h, to], rx.at[way, h, to], st_s.at[way, r], st_r.at[way, r], s, nxt[way])
 
     def row_start(way, r):
         m, h = r // H, lax.rem(r, H)
@@ -373,12 +416,6 @@
         def _():
             part[c, h, to] = (mine(h, to) + rx[way, h, to].astype(F32)).astype(BF16)
             row_hop(way, r).start()
-
-    def each(lo, hi, body):
-        def step(i, carry):
-            body(i)
-            return carry
-        lax.fori_loop(lo, hi, step, 0)
 
     def scatter(h):
         pair_copy(h).wait_recv()
@@ -394,55 +431,35 @@
             for dev in range(n_dev):
                 part[dev % 2, h, dev // 2, :, pl.ds(n * tile, tile)] = value[dev * padded:dev * padded + rows]
         pair_copy(h).start()
+        if h < steps:
+            backward(h)
         if h > 0:
             scatter(h - 1)
 
-    def gx(i):
-        return remote(gtx.at[i], gprx.at[i], gx_s.at[i], gx_r.at[i], s, partner)
-
-    def exchange(which):
-        @pl.when(other == which)
-        def _():
-            for i in range(pieces):
-                gtx[i] = gsum[which, i].astype(BF16)
-                gx(i).start()
-
-    counted = ready
-    backward(done)
+    def rest(r):
+        for way in range(2):
+            @pl.when(hops[way] == 0)
+            def _():
+                row_start(way, r)
+
     scatter(H - 1)
-    for j in range(done + 1, steps):
+    each(H, lead, rest)
+    for j in range(H, steps):
         backward(j)
-    weight_sums(1, 0, steps)
-    exchange(1)
-    weight_sums(0, counted, steps)
-    exchange(0)
+    weight_sums(1, front, pieces)
+    exchange(1, front, pieces)
+    for way in range(2):
+        @pl.when(both(c == 1, hops[way] == 1))
+        def _():
+            for i in range(front):
+                sum_relay(way, i)
+    weight_sums(0, 0, pieces)
+    exchange(0, 0, pieces)
     for h in range(H):
         for way in range(2):
             @pl.when(hops[way] == 1)
             def _():
                 row_relay(way, h)
-
-    def term(i):
-        return gsum[c, i] + gprx[i].astype(F32)
-
-    def sum_hop(way, i):
-        return remote(wtx.at[way, i], wrx.at[way, i], st_s.at[way, H + i], st_r.at[way, H + i], s, nxt[way])
-
-    def sum_first(i):
-        gx(i).wait_recv()
-        for way in range(2):
-            @pl.when(hops[way] == 0)
-            def _():
-                wtx[way, i] = term(i).astype(BF16)
-                sum_hop(way, i).start()
-
-    def sum_relay(way, i):
-        sum_hop(way, i).wait_recv()
-
-        @pl.when(has_next[way])
-        def _():
-            wtx[way, i] = (term(i) + wrx[way, i].astype(F32)).astype(BF16)
-            sum_hop(way, i).start()
 
     def give(i, lane):
         return remote(gout.at[lane, i], gout.at[lane, i], wp_s.at[i], wp_r.at[i], s, partner)
@@ -452,16 +469,13 @@
         gout[c, i] = (value * factor).astype(BF16)
         give(i, c).start()
 
-    each(0, pieces, sum_first)
-
-    def rest(r):
-        for way in range(2):
-            @pl.when(hops[way] == 0)
-            def _():
-                row_start(way, r)
-
-    each(H, far, rest)
-    for j in range(counted, steps):
+    @pl.when(c == 0)
+    def _():
+        each(0, front, sum_first)
+
+    each(front, pieces, sum_first)
+    each(lead, far, rest)
+    for j in range(steps):
         downward(j)
 
     count = far + pieces
@@ -470,21 +484,22 @@
     def slot(t):
         for way in range(2):
             i = t - SKEW * hops[way]
+            moved = c * jnp.minimum(hops[way], 1) * (2 - jnp.minimum(hops[way], 2))
             live = hops[way] > 0
 
-            @pl.when(both(hops[way] > 1, both(i >= 0, i < H)))
+            @pl.when(both(live, both(i >= H * (2 - jnp.minimum(hops[way], 2)), i < lead)))
             def _():
                 row_relay(way, i)
 
-            @pl.when(both(live, both(i >= H, i < H + pieces)))
-            def _():
-                sum_relay(way, i - H)
-
-            @pl.when(both(live, both(i >= H + pieces, i < count)))
+            @pl.when(both(live, both(i >= lead + front * moved, i < lead + pieces)))
+            def _():
+                sum_relay(way, i - lead)
+
+            @pl.when(both(live, both(i >= lead + pieces, i < count)))
             def _():
                 row_relay(way, i - pieces)
 
-        i = t - SKEW * farther - H
+        i = t - SKEW * farther - lead
 
         @pl.when(both(i >= 0, i < pieces))
         def _():
@@ -497,7 +512,7 @@
 
     @pl.when(s > 0)
     def _():
-        for j in range(steps):
+        for j in range(steps + 1):
             grad_copy(j).wait_send()
 
     gather_drain()
@@ -604,7 +619,7 @@
             V((pieces, depth, fe), BF16),
             V((2, pieces, depth, fe), BF16),
             V((2, pieces, depth, fe), BF16),
-            dma((6,)), dma((H,)), dma((H,)), dma((steps,)), dma((steps,)),
+            dma((6,)), dma((H,)), dma((H,)), dma((steps + 1,)), dma((steps + 1,)),
             dma((2, Q - 1, H)), dma((2, Q - 1, H)), dma((2, Q, H)), dma((2, Q, H)),
             dma((H,)), dma((H,)), dma((pieces,)), dma((pieces,)),
             dma((2, count)), dma((2, count)), dma((pieces,)), dma((pieces,)),

time: 59.8 us -> 61.6 us (1.030); the launches traced: 59.6 us -> 60.7 us
  Pallas kernels: 58.9 us -> 59.9 us
    pallas_call x1, Pallas kernels: 57.2 us -> 58.2 us  [shards(): pl.pallas_call(functools.partial(kernel, sections, n_dev, chunk, split),...]
where the time goes in v3:
time: 61.6 us; the launch traced here: 60.7 us
  Pallas kernels  59.9 us (97%)
  between operations  0.8 us (1%)
    pallas_call x1, Pallas kernels, shards(): pl.pallas_call(functools.partial(kernel, sections, n_dev, chunk, split),...  58.2 us
    pallas_call x1, Pallas kernels, shards(): pl.pallas_call(finish, out_shape=(jax.ShapeDtypeStruct((1, rows, cl), BF1...  1.69 us

profile of v3, /device:TPU:5, one launch (start us, length us, event | category | flops | bytes accessed | tf_op | source)
XLA Modules:
  0.0 60.7 jit_solution(528248938962795273)
XLA Ops:
  0.6 58.2 %relay.1 = (bf16[98,1024]{1,0:T(8,128)(2,1)S(1)}, bf16[1568,256]{1,0:T(8,128)(2,1)S(1)}, bf16[2,8,32,1024]{3,2,1,0:T(8,128)(2,1)S(1)}) custom-call(bf16[98,1024]{1,0:T(8,128)(2,1)} %bitcast.13, bf16[98,1024]{1,0:T(8,128)(2,1)} %entry_hbm.1, f32[1,1024]{1,0:T(1,128)} %gain1.1, f32[1,1024]{1,0:T(1,128)} %shift1.1, bf16[1024,512]{1,0:T(8,128)(2,1)} %bitcast.7, ...), custom_call_target="tpu_custom_call" | custom-call | tf_op jit(solution)/shard_map/relay/pallas_call | solution.py:590
  58.9 1.7 %finish.1 = (bf16[1,98,1024]{2,1,0:T(8,128)(2,1)}, bf16[1,1568,256]{2,1,0:T(8,128)(2,1)}, f32[1,256,1024]{2,1,0:T(8,128)}, f32[1,1024,256]{2,1,0:T(8,128)}) custom-call(bf16[98,1024]{1,0:T(8,128)(2,1)S(1)} %get-tuple-element.7.late_in, bf16[1568,256]{1,0:T(8,128)(2,1)S(1)} %get-tuple-element.8.grad_in, bf16[2,8,32,1024]{3,2,1,0:T(8,128)(2,1)S(1)} %get-tuple-element.9.sums), custom_call_target="tpu_custom_call" | custom-call | tf_op jit(solution)/shard_map/finish/pallas_call | solution.py:635

commit v4 on v3

--- a/solution.py
+++ b/solution.py
@@ -11,8 +11,8 @@
 MESH = pl.DeviceIdType.MESH
 epsilon = 1e-05
 H = 4
-SKEW = 3
-LEAD = 2
+SKEW = 5
+LEAD = 1
 F32 = jnp.float32
 BF16 = jnp.bfloat16
 
@@ -35,6 +35,12 @@
 
 def both(a, b):
     return jnp.logical_and(a, b)
+
+
+def cuts(ce):
+    pieces = ce // 16
+    front = pieces // 2
+    return pieces, front, (pieces - front) // 2 + pieces // 2
 
 
 def kernel(
@@ -63,9 +69,10 @@
     total_rows = rows * n_dev
     hid = wexp.shape[1]
     wide = eexp.shape[1]
-    pieces, depth = gsum.shape[1], gsum.shape[2]
     ce = grad.shape[1]
-    front = pieces // 2
+    pieces, front, share = cuts(ce)
+    depth = ce // pieces
+    half_r, half_e = (pieces - front) // 2, pieces // 2
     ahead = front * depth
     factor = 1.0 / math.sqrt(e_rows * n_dev)
 
@@ -186,7 +193,7 @@
         piece = lbuf.at[h, source(way, k) * 2 + c]
         return remote(piece, piece, ag_s.at[way, k - 1, h], ag_r.at[way, k - 1, h], s, nxt[way])
 
-    def share(way, k, h, lane):
+    def lend(way, k, h, lane):
         piece = lbuf.at[h, source(way, k) * 2 + lane]
         return remote(piece, piece, agp_s.at[way, k, h], agp_r.at[way, k, h], s, partner)
 
@@ -203,7 +210,7 @@
             @pl.when(has_next[way])
             def _():
                 hop(way, 0, h).start()
-        share(0, 0, h, c).start()
+        lend(0, 0, h, c).start()
 
     def relay(k, h):
         for way in range(2):
@@ -214,19 +221,19 @@
                     @pl.when(has_next[way])
                     def _():
                         hop(way, k, h).start()
-                share(way, k, h, c).start()
+                lend(way, k, h, c).start()
 
     def gathered(h):
-        share(0, 0, h, other).wait_recv()
+        lend(0, 0, h, other).wait_recv()
         for k in range(1, Q):
             for way in range(2):
                 @pl.when(have(way, k))
                 def _():
-                    share(way, k, h, other).wait_recv()
+                    lend(way, k, h, other).wait_recv()
 
     def gather_drain():
         for h in range(H):
-            share(0, 0, h, c).wait_send()
+            lend(0, 0, h, c).wait_send()
             for way in range(2):
                 @pl.when(has_next[way])
                 def _():
@@ -234,7 +241,7 @@
                 for k in range(1, Q):
                     @pl.when(have(way, k))
                     def _():
-                        share(way, k, h, c).wait_send()
+                        lend(way, k, h, c).wait_send()
                         if k < last:
                             @pl.when(has_next[way])
                             def _():
@@ -252,20 +259,20 @@
 
     def backward(j):
         at = chunk_rows(j)
-        grad_wait(j)
         back = dot(grad[at], ered[...], 1, 1)
         slope[at] = (back * dsl[at].astype(F32)).astype(BF16)
 
     def downward(j):
-        at = chunk_rows(j)
+        at = pl.ds(pl.multiple_of(j * chunk, chunk), chunk)
         input_grad[at] = (grad[at].astype(F32) + dot(slope[at], eexp[...], 1, 1)).astype(BF16)
 
-    def weight_sums(which, lo, hi):
-        a, b = ((saved, slope), (grad, act))[which]
+    def weight_sums(a, b, lo, hi, places):
         at = pl.ds(lo * depth, (hi - lo) * depth)
         for n in range(wide // 256):
             col = pl.ds(n * 256, 256)
-            gsum[which, lo:hi, :, col] = dot(a[:, at], b[:, col], 0, 0).reshape(hi - lo, depth, 256)
+            value = dot(a[:, at], b[:, col], 0, 0).reshape(hi - lo, depth, 256)
+            for start, low, high in places:
+                gsum[start:start + high - low, :, col] = value[low - lo:high - lo]
 
     local[0].wait()
     local[1].wait()
@@ -325,15 +332,15 @@
     def gx(i):
         return remote(gtx.at[i], gprx.at[i], gx_s.at[i], gx_r.at[i], s, partner)
 
-    def exchange(which, lo, hi):
-        @pl.when(other == which)
+    def exchange(lane, lo, hi):
+        @pl.when(other == lane)
         def _():
             for i in range(lo, hi):
-                gtx[i] = gsum[which, i].astype(BF16)
+                gtx[i] = gsum[i + share * lane].astype(BF16)
                 gx(i).start()
 
     def term(i):
-        return gsum[c, i] + gprx[i].astype(F32)
+        return gsum[i + share * c] + gprx[i].astype(F32)
 
     def sum_hop(way, i):
         at = far + i
@@ -370,8 +377,8 @@
         relay(last, h)
         if h == H - 1:
             grad_wait(steps)
-            weight_sums(1, 0, front)
-            exchange(1, 0, front)
+            weight_sums(grad, act, 0, front, ((2 * share, 0, front),))
+            exchange(1, share, share + front)
         if h > 0:
             gathered(h - 1)
             activate(h - 1)
@@ -382,7 +389,7 @@
 
     @pl.when(c == 1)
     def _():
-        each(0, front, sum_first)
+        each(share, share + front, sum_first)
 
     def pair_copy(h):
         return remote(part.at[other, h], prx.at[h], px_s.at[h], px_r.at[h], s, partner)
@@ -408,12 +415,9 @@
         m, h = r // H, lax.rem(r, H)
         to = goal(way, m)
 
-        @pl.when(last - m >= hops[way])
+        @pl.when(last - m > hops[way])
         def _():
             row_hop(way, r).wait_recv()
-
-        @pl.when(last - m > hops[way])
-        def _():
             part[c, h, to] = (mine(h, to) + rx[way, h, to].astype(F32)).astype(BF16)
             row_hop(way, r).start()
 
@@ -432,6 +436,7 @@
                 part[dev % 2, h, dev // 2, :, pl.ds(n * tile, tile)] = value[dev * padded:dev * padded + rows]
         pair_copy(h).start()
         if h < steps:
+            grad_wait(h)
             backward(h)
         if h > 0:
             scatter(h - 1)
@@ -445,65 +450,78 @@
     scatter(H - 1)
     each(H, lead, rest)
     for j in range(H, steps):
+        grad_wait(j)
+    weight_sums(grad, act, front, pieces, ((0, front, front + half_r), (share, front + half_r, pieces)))
+    for lane in range(2):
+        exchange(lane, 0, half_r)
+    for j in range(H, steps):
         backward(j)
-    weight_sums(1, front, pieces)
-    exchange(1, front, pieces)
+    each(0, half_r, sum_first)
     for way in range(2):
         @pl.when(both(c == 1, hops[way] == 1))
         def _():
-            for i in range(front):
-                sum_relay(way, i)
-    weight_sums(0, 0, pieces)
-    exchange(0, 0, pieces)
-    for h in range(H):
-        for way in range(2):
-            @pl.when(hops[way] == 1)
-            def _():
-                row_relay(way, h)
+            each(share, share + front, functools.partial(sum_relay, way))
+    weight_sums(saved, slope, 0, pieces, ((half_r, 0, half_e), (share + half_r, half_e, pieces)))
+    for lane in range(2):
+        exchange(lane, half_r, share)
+    for way in range(2):
+        @pl.when(hops[way] == 1)
+        def _():
+            each(0, H, functools.partial(row_relay, way))
+    for way in range(2):
+        @pl.when(both(c == 1, hops[way] == 2))
+        def _():
+            each(share, share + front, functools.partial(sum_relay, way))
 
     def give(i, lane):
-        return remote(gout.at[lane, i], gout.at[lane, i], wp_s.at[i], wp_r.at[i], s, partner)
+        piece = gout.at[i + share * lane]
+        return remote(piece, piece, wp_s.at[i], wp_r.at[i], s, partner)
 
     def sum_finish(i):
         value = term(i) + (wrx[0, i].astype(F32) + wrx[1, i].astype(F32))
-        gout[c, i] = (value * factor).astype(BF16)
+        gout[i + share * c] = (value * factor).astype(BF16)
         give(i, c).start()
 
-    @pl.when(c == 0)
-    def _():
-        each(0, front, sum_first)
-
-    each(front, pieces, sum_first)
+    each(half_r, share, sum_first)
     each(lead, far, rest)
-    for j in range(steps):
-        downward(j)
-
-    count = far + pieces
+    count = far + share
     farther = jnp.maximum(hops[0], hops[1])
+    calm = H + 2 * SKEW
 
     def slot(t):
         for way in range(2):
             i = t - SKEW * hops[way]
-            moved = c * jnp.minimum(hops[way], 1) * (2 - jnp.minimum(hops[way], 2))
             live = hops[way] > 0
 
-            @pl.when(both(live, both(i >= H * (2 - jnp.minimum(hops[way], 2)), i < lead)))
+            @pl.when(both(hops[way] > 1, both(i >= 0, i < H)))
             def _():
                 row_relay(way, i)
 
-            @pl.when(both(live, both(i >= lead + front * moved, i < lead + pieces)))
-            def _():
-                sum_relay(way, i - lead)
-
-            @pl.when(both(live, both(i >= lead + pieces, i < count)))
-            def _():
-                row_relay(way, i - pieces)
-
-        i = t - SKEW * farther - lead
-
-        @pl.when(both(i >= 0, i < pieces))
+            @pl.when(both(both(c == 1, hops[way] > 2), both(i >= H, i < H + front)))
+            def _():
+                sum_relay(way, i - H + share)
+
+            @pl.when(both(live, both(i >= H, i < H + share)))
+            def _():
+                sum_relay(way, i - H)
+
+            @pl.when(both(live, both(i >= H + share, i < count)))
+            def _():
+                row_relay(way, i - share)
+
+        i = t - SKEW * farther - H
+
+        @pl.when(both(c == 1, both(i >= 0, i < front)))
+        def _():
+            sum_finish(i + share)
+
+        @pl.when(both(i >= 0, i < share))
         def _():
             sum_finish(i)
+
+        @pl.when(both(t >= calm, t < calm + steps))
+        def _():
+            downward(t - calm)
 
     @pl.when(s < sections - 1)
     def _():
@@ -519,9 +537,13 @@
     for h in range(H):
         pair_copy(h).wait_send()
 
-    each(SKEW, count + SKEW * last, slot)
+    each(SKEW, max(count + SKEW * last, calm + steps), slot)
 
     for h in range(H):
+        for way in range(2):
+            @pl.when(hops[way] > 0)
+            def _():
+                row_hop(way, (last - hops[way]) * H + h).wait_recv()
         value = mine(h, q) + rx[0, h, q].astype(F32) + rx[1, h, q].astype(F32)
         late_out[:, cols(h)] = (lbuf[h, d].astype(F32) + value).astype(BF16)
 
@@ -534,16 +556,26 @@
     each(0, far, drain_rows)
 
     def drain_sums(i):
+        give(i, c).wait_send()
+        for way in range(2):
+            @pl.when(has_next[way])
+            def _():
+                sum_hop(way, i).wait_send()
+
+    def drain_pair(i):
         gx(i).wait_send()
-        give(i, c).wait_send()
-        for way in range(2):
-            @pl.when(has_next[way])
-            def _():
-                sum_hop(way, i).wait_send()
-
-    each(0, pieces, drain_sums)
-    for i in range(pieces):
         give(i, other).wait_recv()
+
+    each(0, share, drain_sums)
+    each(0, share, drain_pair)
+
+    @pl.when(c == 1)
+    def _():
+        each(share, share + front, drain_sums)
+
+    @pl.when(c == 0)
+    def _():
+        each(share, share + front, drain_pair)
 
 
 def finish(late_in, grad_in, sums, late_out, input_grad, gexp, gred, wide_e, wide_r, sem):
@@ -552,12 +584,19 @@
     b = pltpu.make_async_copy(late_in, late_out.at[0], sem.at[1])
     a.start()
     b.start()
-    wide_e[...] = sums[0].reshape(ce, fe).astype(F32)
+    pieces, front, share = cuts(ce)
+    depth = ce // pieces
+    half_r = (pieces - front) // 2
+    for lane in range(2):
+        at = pl.ds(lane * (ce // 2), ce // 2)
+        wide_e[at] = sums[lane * share + half_r:lane * share + share].reshape(ce // 2, fe).astype(F32)
     x = pltpu.make_async_copy(wide_e, gexp.at[0], sem.at[2])
     x.start()
     for n in range(fe // 256):
         at = pl.ds(n * 256, 256)
-        wide_r[at, :] = sums[1, :, :, at].reshape(ce, 256).astype(F32).T
+        wide_r[at, 0:front * depth] = sums[2 * share:, :, at].reshape(front * depth, 256).astype(F32).T
+        later = [sums[lane:lane + half_r, :, at].reshape(half_r * depth, 256) for lane in (0, share)]
+        wide_r[at, front * depth:] = jnp.concatenate(later).astype(F32).T
     y = pltpu.make_async_copy(wide_r, gred.at[0], sem.at[3])
     y.start()
     for copy in (a, b, x, y):
@@ -578,9 +617,10 @@
     padded = -(-rows // 16) * 16
     chunk = max(k for k in range(16, 257, 16) if e_rows % k == 0)
     steps = e_rows // chunk
-    pieces = ce // 32
+    pieces, front, share = cuts(ce)
     depth = ce // pieces
-    count = (Q - 1) * H + pieces
+    own = share + front
+    count = (Q - 1) * H + own
     split = n_dev * padded * hid * 4 <= 4 * 1024 * 1024
     hbm = pl.BlockSpec(memory_space=pltpu.HBM)
     any_spec = pl.BlockSpec(memory_space=pl.ANY)
@@ -592,7 +632,7 @@
         out_shape=(
             V((rows, cl), BF16),
             V((e_rows, ce), BF16),
-            V((2, pieces, depth, fe), BF16),
+            V((2 * pieces, depth, fe), BF16),
         ),
         in_specs=[hbm, hbm, vm, vm, hbm, vm, vm] + [hbm] * 6,
         out_specs=(vm, vm, vm),
@@ -614,15 +654,15 @@
             V((e_rows, fe), BF16),
             V((e_rows, fe), BF16),
             V((e_rows, fe), BF16),
-            V((2, pieces, depth, fe), F32),
-            V((pieces, depth, fe), BF16),
-            V((pieces, depth, fe), BF16),
-            V((2, pieces, depth, fe), BF16),
-            V((2, pieces, depth, fe), BF16),
+            V((2 * pieces, depth, fe), F32),
+            V((own, depth, fe), BF16),
+            V((own, depth, fe), BF16),
+            V((2, own, depth, fe), BF16),
+            V((2, own, depth, fe), BF16),
             dma((6,)), dma((H,)), dma((H,)), dma((steps + 1,)), dma((steps + 1,)),
             dma((2, Q - 1, H)), dma((2, Q - 1, H)), dma((2, Q, H)), dma((2, Q, H)),
-            dma((H,)), dma((H,)), dma((pieces,)), dma((pieces,)),
-            dma((2, count)), dma((2, count)), dma((pieces,)), dma((pieces,)),
+            dma((H,)), dma((H,)), dma((own,)), dma((own,)),
+            dma((2, count)), dma((2, count)), dma((own,)), dma((own,)),
         ],
         compiler_params=pltpu.CompilerParams(
             collective_id=0, has_side_effects=True, vmem_limit_bytes=60 * 1024 * 1024

time: 61.6 us -> 59.2 us (0.961); the launches traced: 60.7 us -> 59 us
  Pallas kernels: 59.9 us -> 58.4 us
    pallas_call x1, Pallas kernels: 58.2 us -> 56.7 us  [shards(): pl.pallas_call(functools.partial(kernel, sections, n_dev, chunk, split),...]
where the time goes in v4:
time: 59.2 us; the launch traced here: 59 us
  Pallas kernels  58.4 us (99%)
  between operations  0.64 us (1%)
    pallas_call x1, Pallas kernels, shards(): pl.pallas_call(functools.partial(kernel, sections, n_dev, chunk, split),...  56.7 us
    pallas_call x1, Pallas kernels, shards(): pl.pallas_call(finish, out_shape=(jax.ShapeDtypeStruct((1, rows, cl), BF1...  1.69 us

profile of v4, /device:TPU:5, one launch (start us, length us, event | category | flops | bytes accessed | tf_op | source)
XLA Modules:
  0.0 59.0 jit_solution(2387201859869923937)
XLA Ops:
  0.6 56.7 %relay.1 = (bf16[98,1024]{1,0:T(8,128)(2,1)S(1)}, bf16[1568,256]{1,0:T(8,128)(2,1)S(1)}, bf16[32,16,1024]{2,1,0:T(8,128)(2,1)S(1)}) custom-call(bf16[98,1024]{1,0:T(8,128)(2,1)} %bitcast.13, bf16[98,1024]{1,0:T(8,128)(2,1)} %entry_hbm.1, f32[1,1024]{1,0:T(1,128)} %gain1.1, f32[1,1024]{1,0:T(1,128)} %shift1.1, bf16[1024,512]{1,0:T(8,128)(2,1)} %bitcast.7, ...), custom_call_target="tpu_custom_call" | custom-call | tf_op jit(solution)/shard_map/relay/pallas_call | solution.py:630
  57.3 1.7 %finish.1 = (bf16[1,98,1024]{2,1,0:T(8,128)(2,1)}, bf16[1,1568,256]{2,1,0:T(8,128)(2,1)}, f32[1,256,1024]{2,1,0:T(8,128)}, f32[1,1024,256]{2,1,0:T(8,128)}) custom-call(bf16[98,1024]{1,0:T(8,128)(2,1)S(1)} %get-tuple-element.7.late_in, bf16[1568,256]{1,0:T(8,128)(2,1)S(1)} %get-tuple-element.8.grad_in, bf16[32,16,1024]{2,1,0:T(8,128)(2,1)S(1)} %get-tuple-element.9.sums), custom_call_target="tpu_custom_call" | custom-call | tf_op jit(solution)/shard_map/finish/pallas_call | solution.py:675

commit v5 on v4

--- a/solution.py
+++ b/solution.py
@@ -11,8 +11,10 @@
 MESH = pl.DeviceIdType.MESH
 epsilon = 1e-05
 H = 4
-SKEW = 5
-LEAD = 1
+U = 2
+SKEW = 4
+LEAD = 0
+LAG = 3
 F32 = jnp.float32
 BF16 = jnp.bfloat16
 
@@ -118,14 +120,23 @@
     def cols(h):
         return pl.ds(h * half, half)
 
-    def late_copy(h):
+    fine = half // U
+    G = H * U
+
+    def fine_cols(g):
+        return pl.ds(g * fine, fine)
+
+    def rows_of(g, dev):
+        return lbuf.at[g // U, dev, :, pl.ds(g % U * fine, fine)]
+
+    def late_copy(g):
         return remote(
-            stage.at[:, cols(h)], lbuf.at[h, d], perm_send.at[h], perm_recv.at[h],
+            stage.at[:, fine_cols(g)], rows_of(g, d), perm_send.at[g], perm_recv.at[g],
             jnp.minimum(s + 1, sections - 1), d,
         )
 
-    def entry_copy(h):
-        return pltpu.make_async_copy(entry_hbm.at[:, cols(h)], lbuf.at[h, d], perm_recv.at[h])
+    def entry_copy(g):
+        return pltpu.make_async_copy(entry_hbm.at[:, fine_cols(g)], rows_of(g, d), perm_recv.at[g])
 
     def chunk_rows(j):
         return pl.ds(j * chunk, chunk)
@@ -161,13 +172,13 @@
 
     @pl.when(s < sections - 1)
     def _():
-        for h in range(H):
-            late_copy(h).start()
+        for g in range(G):
+            late_copy(g).start()
 
     @pl.when(s == 0)
     def _():
-        for h in range(H):
-            entry_copy(h).start()
+        for g in range(G):
+            entry_copy(g).start()
 
     @pl.when(s > 0)
     def _():
@@ -186,15 +197,15 @@
         return hops[way] >= k
 
     def hop(way, k, h):
-        piece = lbuf.at[h, source(way, k) * 2 + c]
+        piece = rows_of(h, source(way, k) * 2 + c)
         return remote(piece, piece, ag_s.at[way, k, h], ag_r.at[way, k, h], s, nxt[way])
 
     def arrival(way, k, h):
-        piece = lbuf.at[h, source(way, k) * 2 + c]
+        piece = rows_of(h, source(way, k) * 2 + c)
         return remote(piece, piece, ag_s.at[way, k - 1, h], ag_r.at[way, k - 1, h], s, nxt[way])
 
     def lend(way, k, h, lane):
-        piece = lbuf.at[h, source(way, k) * 2 + lane]
+        piece = rows_of(h, source(way, k) * 2 + lane)
         return remote(piece, piece, agp_s.at[way, k, h], agp_r.at[way, k, h], s, partner)
 
     def own(h):
@@ -224,15 +235,16 @@
                 lend(way, k, h, c).start()
 
     def gathered(h):
-        lend(0, 0, h, other).wait_recv()
-        for k in range(1, Q):
-            for way in range(2):
-                @pl.when(have(way, k))
-                def _():
-                    lend(way, k, h, other).wait_recv()
+        for g in range(h * U, h * U + U):
+            lend(0, 0, g, other).wait_recv()
+            for k in range(1, Q):
+                for way in range(2):
+                    @pl.when(have(way, k))
+                    def _():
+                        lend(way, k, g, other).wait_recv()
 
     def gather_drain():
-        for h in range(H):
+        for h in range(G):
             lend(0, 0, h, c).wait_send()
             for way in range(2):
                 @pl.when(has_next[way])
@@ -286,11 +298,11 @@
         def _():
             wrx[way] = jnp.zeros(wrx.shape[1:], BF16)
             rx[way] = jnp.zeros(rx.shape[1:], BF16)
-    for h in range(H):
-        own(h)
-        if early + h < steps:
-            forward(early + h)
-    for j in range(early + H, steps):
+    for g in range(G):
+        own(g)
+        if early + g < steps:
+            forward(early + g)
+    for j in range(early + G, steps):
         forward(j)
     local[2].wait()
     local[3].wait()
@@ -371,10 +383,11 @@
     far = last * H
     lead = min(H + LEAD, far)
     for k in range(1, last):
-        for h in range(H):
-            relay(k, h)
+        for g in range(G):
+            relay(k, g)
     for h in range(H):
-        relay(last, h)
+        for g in range(h * U, h * U + U):
+            relay(last, g)
         if h == H - 1:
             grad_wait(steps)
             weight_sums(grad, act, 0, front, ((2 * share, 0, front),))
@@ -464,14 +477,22 @@
     weight_sums(saved, slope, 0, pieces, ((half_r, 0, half_e), (share + half_r, half_e, pieces)))
     for lane in range(2):
         exchange(lane, half_r, share)
+    per = front // H
+    for h in range(H):
+        for way in range(2):
+            @pl.when(both(c == 1, hops[way] == 2))
+            def _():
+                for i in range(per):
+                    sum_relay(way, share + h * per + i)
+        for way in range(2):
+            @pl.when(hops[way] == 1)
+            def _():
+                row_relay(way, h)
     for way in range(2):
-        @pl.when(hops[way] == 1)
-        def _():
-            each(0, H, functools.partial(row_relay, way))
-    for way in range(2):
-        @pl.when(both(c == 1, hops[way] == 2))
-        def _():
-            each(share, share + front, functools.partial(sum_relay, way))
+        @pl.when(hops[way] == 2)
+        def _():
+            for h in range(H // 2):
+                row_relay(way, h)
 
     def give(i, lane):
         piece = gout.at[i + share * lane]
@@ -488,12 +509,29 @@
     farther = jnp.maximum(hops[0], hops[1])
     calm = H + 2 * SKEW
 
+    def drain_gifts(i):
+        give(i, c).wait_send()
+
+    def drain_sums(i):
+        @pl.when(i < share)
+        def _():
+            give(i, c).wait_send()
+
+        for way in range(2):
+            @pl.when(has_next[way])
+            def _():
+                sum_hop(way, i).wait_send()
+
+    def drain_pair(i):
+        gx(i).wait_send()
+        give(i, other).wait_recv()
+
     def slot(t):
         for way in range(2):
             i = t - SKEW * hops[way]
             live = hops[way] > 0
 
-            @pl.when(both(hops[way] > 1, both(i >= 0, i < H)))
+            @pl.when(both(hops[way] > 1, both(i >= H // 2 * (3 - jnp.minimum(hops[way], 3)), i < H)))
             def _():
                 row_relay(way, i)
 
@@ -514,19 +552,25 @@
         @pl.when(both(c == 1, both(i >= 0, i < front)))
         def _():
             sum_finish(i + share)
+            drain_sums(i + share)
 
         @pl.when(both(i >= 0, i < share))
         def _():
             sum_finish(i)
 
+        @pl.when(both(i >= LAG, i < share))
+        def _():
+            drain_sums(i - LAG)
+            drain_pair(i - LAG)
+
         @pl.when(both(t >= calm, t < calm + steps))
         def _():
             downward(t - calm)
 
     @pl.when(s < sections - 1)
     def _():
-        for h in range(H):
-            late_copy(h).wait_send()
+        for g in range(G):
+            late_copy(g).wait_send()
 
     @pl.when(s > 0)
     def _():
@@ -537,7 +581,7 @@
     for h in range(H):
         pair_copy(h).wait_send()
 
-    each(SKEW, max(count + SKEW * last, calm + steps), slot)
+    each(SKEW, max(H + share + SKEW * last, calm + steps), slot)
 
     for h in range(H):
         for way in range(2):
@@ -555,23 +599,12 @@
 
     each(0, far, drain_rows)
 
-    def drain_sums(i):
-        give(i, c).wait_send()
-        for way in range(2):
-            @pl.when(has_next[way])
-            def _():
-                sum_hop(way, i).wait_send()
-
-    def drain_pair(i):
-        gx(i).wait_send()
-        give(i, other).wait_recv()
-
-    each(0, share, drain_sums)
-    each(0, share, drain_pair)
+    each(share - LAG, share, drain_sums)
+    each(share - LAG, share, drain_pair)
 
     @pl.when(c == 1)
     def _():
-        each(share, share + front, drain_sums)
+        each(share, share + front, drain_gifts)
 
     @pl.when(c == 0)
     def _():
@@ -587,19 +620,23 @@
     pieces, front, share = cuts(ce)
     depth = ce // pieces
     half_r = (pieces - front) // 2
+    copies = [a, b]
+
+    def send(src, dst):
+        copies.append(pltpu.make_async_copy(src, dst, sem.at[len(copies)]))
+        copies[-1].start()
+
     for lane in range(2):
         at = pl.ds(lane * (ce // 2), ce // 2)
         wide_e[at] = sums[lane * share + half_r:lane * share + share].reshape(ce // 2, fe).astype(F32)
-    x = pltpu.make_async_copy(wide_e, gexp.at[0], sem.at[2])
-    x.start()
+        send(wide_e.at[at], gexp.at[0, at])
     for n in range(fe // 256):
         at = pl.ds(n * 256, 256)
         wide_r[at, 0:front * depth] = sums[2 * share:, :, at].reshape(front * depth, 256).astype(F32).T
         later = [sums[lane:lane + half_r, :, at].reshape(half_r * depth, 256) for lane in (0, share)]
         wide_r[at, front * depth:] = jnp.concatenate(later).astype(F32).T
-    y = pltpu.make_async_copy(wide_r, gred.at[0], sem.at[3])
-    y.start()
-    for copy in (a, b, x, y):
+        send(wide_r.at[at], gred.at[0, at])
+    for copy in copies:
         copy.wait()
 
 
@@ -659,8 +696,8 @@
             V((own, depth, fe), BF16),
             V((2, own, depth, fe), BF16),
             V((2, own, depth, fe), BF16),
-            dma((6,)), dma((H,)), dma((H,)), dma((steps + 1,)), dma((steps + 1,)),
-            dma((2, Q - 1, H)), dma((2, Q - 1, H)), dma((2, Q, H)), dma((2, Q, H)),
+            dma((6,)), dma((H * U,)), dma((H * U,)), dma((steps + 1,)), dma((steps + 1,)),
+            dma((2, Q - 1, H * U)), dma((2, Q - 1, H * U)), dma((2, Q, H * U)), dma((2, Q, H * U)),
             dma((H,)), dma((H,)), dma((own,)), dma((own,)),
             dma((2, count)), dma((2, count)), dma((own,)), dma((own,)),
         ],
@@ -682,7 +719,7 @@
         ),
         in_specs=[vm, vm, vm],
         out_specs=(any_spec,) * 4,
-        scratch_shapes=[V((ce, fe), F32), V((fe, ce), F32), dma((4,))],
+        scratch_shapes=[V((ce, fe), F32), V((fe, ce), F32), dma((4 + fe // 256,))],
         compiler_params=pltpu.CompilerParams(vmem_limit_bytes=16 * 1024 * 1024),
         name="finish",
     )(late_out, input_grad, sums)

time: 59.2 us -> 59.6 us (level); the launches traced: 59 us -> 58.6 us
  Pallas kernels: 58.4 us -> 57.8 us
    pallas_call x1, Pallas kernels: 56.7 us -> 56.1 us  [shards(): pl.pallas_call(functools.partial(kernel, sections, n_dev, chunk, split),...]
where the time goes in v5:
time: 59.6 us; the launch traced here: 58.6 us
  Pallas kernels  57.8 us (97%)
  between operations  0.8 us (1%)
    pallas_call x1, Pallas kernels, shards(): pl.pallas_call(functools.partial(kernel, sections, n_dev, chunk, split),...  56.1 us
    pallas_call x1, Pallas kernels, shards(): pl.pallas_call(finish, out_shape=(jax.ShapeDtypeStruct((1, rows, cl), BF1...  1.71 us

profile of v5, /device:TPU:5, one launch (start us, length us, event | category | flops | bytes accessed | tf_op | source)
XLA Modules:
  0.0 58.6 jit_solution(17671951337453310312)
XLA Ops:
  0.6 56.1 %relay.1 = (bf16[98,1024]{1,0:T(8,128)(2,1)S(1)}, bf16[1568,256]{1,0:T(8,128)(2,1)S(1)}, bf16[32,16,1024]{2,1,0:T(8,128)(2,1)S(1)}) custom-call(bf16[98,1024]{1,0:T(8,128)(2,1)} %bitcast.13, bf16[98,1024]{1,0:T(8,128)(2,1)} %entry_hbm.1, f32[1,1024]{1,0:T(1,128)} %gain1.1, f32[1,1024]{1,0:T(1,128)} %shift1.1, bf16[1024,512]{1,0:T(8,128)(2,1)} %bitcast.7, ...), custom_call_target="tpu_custom_call" | custom-call | tf_op jit(solution)/shard_map/relay/pallas_call | solution.py:667
  56.7 1.7 %finish.1 = (bf16[1,98,1024]{2,1,0:T(8,128)(2,1)}, bf16[1,1568,256]{2,1,0:T(8,128)(2,1)}, f32[1,256,1024]{2,1,0:T(8,128)}, f32[1,1024,256]{2,1,0:T(8,128)}) custom-call(bf16[98,1024]{1,0:T(8,128)(2,1)S(1)} %get-tuple-element.7.late_in, bf16[1568,256]{1,0:T(8,128)(2,1)S(1)} %get-tuple-element.8.grad_in, bf16[32,16,1024]{2,1,0:T(8,128)(2,1)S(1)} %get-tuple-element.9.sums), custom_call_target="tpu_custom_call" | custom-call | tf_op jit(solution)/shard_map/finish/pallas_call | solution.py:712

commit v6 on v5

--- a/solution.py
+++ b/solution.py
@@ -14,7 +14,6 @@
 U = 2
 SKEW = 4
 LEAD = 0
-LAG = 3
 F32 = jnp.float32
 BF16 = jnp.bfloat16
 
@@ -47,14 +46,14 @@
 
 def kernel(
     sections, n_dev, chunk, split,
-    late_hbm, entry_hbm, gain1, shift1, wexp_hbm, gain2, shift2, wred_hbm,
+    late_hbm, entry_hbm, gain1_hbm, shift1_hbm, wexp_hbm, gain2_hbm, shift2_hbm, wred_hbm,
     saved_hbm, up_hbm, exit_hbm, eexp_hbm, ered_hbm,
     late_out, input_grad, gout,
     stage, lbuf, first, inner, hidden, part, prx, rx,
     wexp, wred, saved, grad, eexp, ered, act, dsl, slope,
-    gsum, gtx, gprx, wtx, wrx,
-    loc_sem, perm_send, perm_recv, gp_send, gp_recv,
-    ag_s, ag_r, agp_s, agp_r, px_s, px_r, gx_s, gx_r, st_s, st_r, wp_s, wp_r,
+    gsum, gtx, gprx, wtx, wrx, gain1, shift1, gain2, shift2,
+    loc_sem, perm_recv, gp_recv, ag_r, agp_r, px_r, gx_r, row_r, sum_r, wp_r,
+    perm_send, gp_send, ag_s, agp_s, px_s, gx_s, row_s, sum_s, wp_s,
 ):
     Q = n_dev // 2
     s = lax.axis_index("section")
@@ -100,12 +99,15 @@
     def _():
         pl.semaphore_signal(barrier, inc=1, device_id=(s + 1, d), device_id_type=MESH)
 
-    stage_copy = pltpu.make_async_copy(late_hbm, stage, loc_sem.at[5])
+    stage_copy = pltpu.make_async_copy(late_hbm, stage, loc_sem.at[9])
     stage_copy.start()
     local = [
         pltpu.make_async_copy(src, dst, loc_sem.at[i])
         for i, (src, dst) in enumerate(
-            ((saved_hbm, saved), (eexp_hbm, eexp), (ered_hbm, ered), (wexp_hbm, wexp), (wred_hbm, wred))
+            (
+                (saved_hbm, saved), (eexp_hbm, eexp), (ered_hbm, ered), (wexp_hbm, wexp), (wred_hbm, wred),
+                (gain1_hbm, gain1), (shift1_hbm, shift1), (gain2_hbm, gain2), (shift2_hbm, shift2),
+            )
         )
     ]
     for copy in local:
@@ -131,7 +133,7 @@
 
     def late_copy(g):
         return remote(
-            stage.at[:, fine_cols(g)], rows_of(g, d), perm_send.at[g], perm_recv.at[g],
+            stage.at[:, fine_cols(g)], rows_of(g, d), perm_send, perm_recv.at[g],
             jnp.minimum(s + 1, sections - 1), d,
         )
 
@@ -148,7 +150,7 @@
 
     def grad_copy(j):
         return remote(
-            up_hbm.at[grad_at(j)], grad.at[grad_at(j)], gp_send.at[j], gp_recv.at[j],
+            up_hbm.at[grad_at(j)], grad.at[grad_at(j)], gp_send, gp_recv.at[j],
             jnp.maximum(s - 1, 0), d,
         )
 
@@ -198,15 +200,15 @@
 
     def hop(way, k, h):
         piece = rows_of(h, source(way, k) * 2 + c)
-        return remote(piece, piece, ag_s.at[way, k, h], ag_r.at[way, k, h], s, nxt[way])
+        return remote(piece, piece, ag_s.at[way], ag_r.at[way, k, h], s, nxt[way])
 
     def arrival(way, k, h):
         piece = rows_of(h, source(way, k) * 2 + c)
-        return remote(piece, piece, ag_s.at[way, k - 1, h], ag_r.at[way, k - 1, h], s, nxt[way])
+        return remote(piece, piece, ag_s.at[way], ag_r.at[way, k - 1, h], s, nxt[way])
 
     def lend(way, k, h, lane):
         piece = rows_of(h, source(way, k) * 2 + lane)
-        return remote(piece, piece, agp_s.at[way, k, h], agp_r.at[way, k, h], s, partner)
+        return remote(piece, piece, agp_s, agp_r.at[h // U], s, partner)
 
     def own(h):
         @pl.when(s == 0)
@@ -234,30 +236,19 @@
                         hop(way, k, h).start()
                 lend(way, k, h, c).start()
 
+    def span(buf, send, recv):
+        return remote(buf, buf, send, recv, s, partner)
+
     def gathered(h):
-        for g in range(h * U, h * U + U):
-            lend(0, 0, g, other).wait_recv()
-            for k in range(1, Q):
-                for way in range(2):
-                    @pl.when(have(way, k))
-                    def _():
-                        lend(way, k, g, other).wait_recv()
+        span(lbuf.at[h, 0:Q], agp_s, agp_r.at[h]).wait_recv()
 
     def gather_drain():
-        for h in range(G):
-            lend(0, 0, h, c).wait_send()
-            for way in range(2):
-                @pl.when(has_next[way])
+        span(lbuf.at[:, 0:Q], agp_s, agp_r.at[0]).wait_send()
+        for way in range(2):
+            for k in range(last):
+                @pl.when(hops[way] == k)
                 def _():
-                    hop(way, 0, h).wait_send()
-                for k in range(1, Q):
-                    @pl.when(have(way, k))
-                    def _():
-                        lend(way, k, h, c).wait_send()
-                        if k < last:
-                            @pl.when(has_next[way])
-                            def _():
-                                hop(way, k, h).wait_send()
+                    span(lbuf.at[:, 0:k + 1], ag_s.at[way], agp_r.at[0]).wait_send()
 
     def forward(j):
         at = chunk_rows(j)
@@ -304,9 +295,8 @@
             forward(early + g)
     for j in range(early + G, steps):
         forward(j)
-    local[2].wait()
-    local[3].wait()
-    local[4].wait()
+    for copy in local[2:]:
+        copy.wait()
 
     def activate(h):
         total = jnp.zeros((1, half), F32)
@@ -341,25 +331,30 @@
                 )
                 hidden[:, at] = scaled_silu(value, spread, offset).astype(BF16)
 
-    def gx(i):
-        return remote(gtx.at[i], gprx.at[i], gx_s.at[i], gx_r.at[i], s, partner)
-
-    def exchange(lane, lo, hi):
+    groups = ((0, half_r), (half_r, half_r + half_e // 2), (half_r + half_e // 2, share), (share, share + front))
+
+    def swap(n):
+        lo, hi = groups[n]
+        return remote(gtx.at[lo:hi], gprx.at[lo:hi], gx_s, gx_r.at[n], s, partner)
+
+    def exchange(lane, n):
         @pl.when(other == lane)
         def _():
-            for i in range(lo, hi):
+            for i in range(*groups[n]):
                 gtx[i] = gsum[i + share * lane].astype(BF16)
-                gx(i).start()
+            swap(n).start()
+
+    def met(n):
+        swap(n).wait_recv()
+        each(*groups[n], sum_first)
 
     def term(i):
         return gsum[i + share * c] + gprx[i].astype(F32)
 
     def sum_hop(way, i):
-        at = far + i
-        return remote(wtx.at[way, i], wrx.at[way, i], st_s.at[way, at], st_r.at[way, at], s, nxt[way])
+        return remote(wtx.at[way, i], wrx.at[way, i], sum_s.at[way], sum_r.at[way, i], s, nxt[way])
 
     def sum_first(i):
-        gx(i).wait_recv()
         for way in range(2):
             @pl.when(hops[way] == 0)
             def _():
@@ -391,7 +386,7 @@
         if h == H - 1:
             grad_wait(steps)
             weight_sums(grad, act, 0, front, ((2 * share, 0, front),))
-            exchange(1, share, share + front)
+            exchange(1, 3)
         if h > 0:
             gathered(h - 1)
             activate(h - 1)
@@ -402,10 +397,10 @@
 
     @pl.when(c == 1)
     def _():
-        each(share, share + front, sum_first)
+        met(3)
 
     def pair_copy(h):
-        return remote(part.at[other, h], prx.at[h], px_s.at[h], px_r.at[h], s, partner)
+        return remote(part.at[other, h], prx.at[h], px_s, px_r.at[h], s, partner)
 
     def mine(h, chip):
         return part[c, h, chip].astype(F32) + prx[h, chip].astype(F32)
@@ -416,7 +411,7 @@
     def row_hop(way, r):
         m, h = r // H, lax.rem(r, H)
         to = goal(way, m)
-        return remote(part.at[c, h, to], rx.at[way, h, to], st_s.at[way, r], st_r.at[way, r], s, nxt[way])
+        return remote(part.at[c, h, to], rx.at[way, h, to], row_s.at[way], row_r.at[way, r], s, nxt[way])
 
     def row_start(way, r):
         m, h = r // H, lax.rem(r, H)
@@ -466,17 +461,18 @@
         grad_wait(j)
     weight_sums(grad, act, front, pieces, ((0, front, front + half_r), (share, front + half_r, pieces)))
     for lane in range(2):
-        exchange(lane, 0, half_r)
+        exchange(lane, 0)
     for j in range(H, steps):
         backward(j)
-    each(0, half_r, sum_first)
+    met(0)
     for way in range(2):
         @pl.when(both(c == 1, hops[way] == 1))
         def _():
             each(share, share + front, functools.partial(sum_relay, way))
     weight_sums(saved, slope, 0, pieces, ((half_r, 0, half_e), (share + half_r, half_e, pieces)))
     for lane in range(2):
-        exchange(lane, half_r, share)
+        exchange(lane, 1)
+        exchange(lane, 2)
     per = front // H
     for h in range(H):
         for way in range(2):
@@ -496,36 +492,20 @@
 
     def give(i, lane):
         piece = gout.at[i + share * lane]
-        return remote(piece, piece, wp_s.at[i], wp_r.at[i], s, partner)
+        return remote(piece, piece, wp_s, wp_r, s, partner)
 
     def sum_finish(i):
         value = term(i) + (wrx[0, i].astype(F32) + wrx[1, i].astype(F32))
         gout[i + share * c] = (value * factor).astype(BF16)
         give(i, c).start()
 
-    each(half_r, share, sum_first)
+    met(1)
+    met(2)
     each(lead, far, rest)
     count = far + share
     farther = jnp.maximum(hops[0], hops[1])
     calm = H + 2 * SKEW
 
-    def drain_gifts(i):
-        give(i, c).wait_send()
-
-    def drain_sums(i):
-        @pl.when(i < share)
-        def _():
-            give(i, c).wait_send()
-
-        for way in range(2):
-            @pl.when(has_next[way])
-            def _():
-                sum_hop(way, i).wait_send()
-
-    def drain_pair(i):
-        gx(i).wait_send()
-        give(i, other).wait_recv()
-
     def slot(t):
         for way in range(2):
             i = t - SKEW * hops[way]
@@ -552,34 +532,31 @@
         @pl.when(both(c == 1, both(i >= 0, i < front)))
         def _():
             sum_finish(i + share)
-            drain_sums(i + share)
 
         @pl.when(both(i >= 0, i < share))
         def _():
             sum_finish(i)
 
-        @pl.when(both(i >= LAG, i < share))
-        def _():
-            drain_sums(i - LAG)
-            drain_pair(i - LAG)
-
         @pl.when(both(t >= calm, t < calm + steps))
         def _():
             downward(t - calm)
 
     @pl.when(s < sections - 1)
     def _():
-        for g in range(G):
-            late_copy(g).wait_send()
+        span(stage, perm_send, perm_recv.at[0]).wait_send()
 
     @pl.when(s > 0)
     def _():
-        for j in range(steps + 1):
-            grad_copy(j).wait_send()
+        remote(up_hbm, grad, gp_send, gp_recv.at[0], s, partner).wait_send()
 
     gather_drain()
-    for h in range(H):
-        pair_copy(h).wait_send()
+    span(prx, px_s, px_r.at[0]).wait_send()
+    for lane in range(2):
+        mass = share + front * lane
+
+        @pl.when(other == lane)
+        def _():
+            span(gtx.at[0:mass], gx_s, gx_r.at[0]).wait_send()
 
     each(SKEW, max(H + share + SKEW * last, calm + steps), slot)
 
@@ -591,24 +568,26 @@
         value = mine(h, q) + rx[0, h, q].astype(F32) + rx[1, h, q].astype(F32)
         late_out[:, cols(h)] = (lbuf[h, d].astype(F32) + value).astype(BF16)
 
-    def drain_rows(r):
-        for way in range(2):
-            @pl.when(last - r // H > hops[way])
-            def _():
-                row_hop(way, r).wait_send()
-
-    each(0, far, drain_rows)
-
-    each(share - LAG, share, drain_sums)
-    each(share - LAG, share, drain_pair)
-
-    @pl.when(c == 1)
-    def _():
-        each(share, share + front, drain_gifts)
-
-    @pl.when(c == 0)
-    def _():
-        each(share, share + front, drain_pair)
+    for way in range(2):
+        for k in range(last):
+            @pl.when(hops[way] == k)
+            def _():
+                span(prx.at[:, 0:last - k], row_s.at[way], px_r.at[0]).wait_send()
+    for lane in range(2):
+        mass = share + front * lane
+        block = gout.at[lane * share:lane * share + mass]
+
+        @pl.when(c == lane)
+        def _():
+            for way in range(2):
+                @pl.when(has_next[way])
+                def _():
+                    span(wtx.at[way, 0:mass], sum_s.at[way], gx_r.at[0]).wait_send()
+            span(block, wp_s, wp_r).wait_send()
+
+        @pl.when(other == lane)
+        def _():
+            span(block, wp_s, wp_r).wait_recv()
 
 
 def finish(late_in, grad_in, sums, late_out, input_grad, gexp, gred, wide_e, wide_r, sem):
@@ -657,7 +636,6 @@
     pieces, front, share = cuts(ce)
     depth = ce // pieces
     own = share + front
-    count = (Q - 1) * H + own
     split = n_dev * padded * hid * 4 <= 4 * 1024 * 1024
     hbm = pl.BlockSpec(memory_space=pltpu.HBM)
     any_spec = pl.BlockSpec(memory_space=pl.ANY)
@@ -671,7 +649,7 @@
             V((e_rows, ce), BF16),
             V((2 * pieces, depth, fe), BF16),
         ),
-        in_specs=[hbm, hbm, vm, vm, hbm, vm, vm] + [hbm] * 6,
+        in_specs=[hbm] * 13,
         out_specs=(vm, vm, vm),
         scratch_shapes=[
             V((rows, cl), BF16),
@@ -696,10 +674,13 @@
             V((own, depth, fe), BF16),
             V((2, own, depth, fe), BF16),
             V((2, own, depth, fe), BF16),
-            dma((6,)), dma((H * U,)), dma((H * U,)), dma((steps + 1,)), dma((steps + 1,)),
-            dma((2, Q - 1, H * U)), dma((2, Q - 1, H * U)), dma((2, Q, H * U)), dma((2, Q, H * U)),
-            dma((H,)), dma((H,)), dma((own,)), dma((own,)),
-            dma((2, count)), dma((2, count)), dma((own,)), dma((own,)),
+            V((1, cl), F32),
+            V((1, cl), F32),
+            V((1, hid), F32),
+            V((1, hid), F32),
+            dma((10,)), dma((H * U,)), dma((steps + 1,)), dma((2, Q - 1, H * U)), dma((H,)), dma((H,)),
+            dma((4,)), dma((2, (Q - 1) * H)), dma((2, own)), dma,
+            dma, dma, dma((2,)), dma, dma, dma, dma((2,)), dma((2,)), dma,
         ],
         compiler_params=pltpu.CompilerParams(
             collective_id=0, has_side_effects=True, vmem_limit_bytes=60 * 1024 * 1024

time: 59.6 us -> 55.6 us (0.933)
  Pallas kernels: 57.8 us -> 54 us
    pallas_call x1, Pallas kernels: 56.1 us -> 52.3 us  [shards(): pl.pallas_call(functools.partial(kernel, sections, n_dev, chunk, split),...]
where the time goes in v6:
time: 55.6 us; the launch traced here: 54.8 us
  Pallas kernels  54 us (97%)
  between operations  0.8 us (1%)
    pallas_call x1, Pallas kernels, shards(): pl.pallas_call(functools.partial(kernel, sections, n_dev, chunk, split),...  52.3 us
    pallas_call x1, Pallas kernels, shards(): pl.pallas_call(finish, out_shape=(jax.ShapeDtypeStruct((1, rows, cl), BF1...  1.71 us

profile of v6, /device:TPU:5, one launch (start us, length us, event | category | flops | bytes accessed | tf_op | source)
XLA Modules:
  0.0 54.8 jit_solution(2055398086270445814)
XLA Ops:
  0.6 52.3 %relay.1 = (bf16[98,1024]{1,0:T(8,128)(2,1)S(1)}, bf16[1568,256]{1,0:T(8,128)(2,1)S(1)}, bf16[32,16,1024]{2,1,0:T(8,128)(2,1)S(1)}) custom-call(bf16[98,1024]{1,0:T(8,128)(2,1)} %bitcast.13, bf16[98,1024]{1,0:T(8,128)(2,1)} %entry_hbm.1, f32[1,1024]{1,0:T(1,128)} %gain1_hbm.1, f32[1,1024]{1,0:T(1,128)} %shift1_hbm.1, bf16[1024,512]{1,0:T(8,128)(2,1)} %bitcast.7, ...), custom_call_target="tpu_custom_call" | custom-call | tf_op jit(solution)/shard_map/relay/pallas_call | solution.py:645
  52.9 1.7 %finish.1 = (bf16[1,98,1024]{2,1,0:T(8,128)(2,1)}, bf16[1,1568,256]{2,1,0:T(8,128)(2,1)}, f32[1,256,1024]{2,1,0:T(8,128)}, f32[1,1024,256]{2,1,0:T(8,128)}) custom-call(bf16[98,1024]{1,0:T(8,128)(2,1)S(1)} %get-tuple-element.7.late_in, bf16[1568,256]{1,0:T(8,128)(2,1)S(1)} %get-tuple-element.8.grad_in, bf16[32,16,1024]{2,1,0:T(8,128)(2,1)S(1)} %get-tuple-element.9.sums), custom_call_target="tpu_custom_call" | custom-call | tf_op jit(solution)/shard_map/finish/pallas_call | solution.py:693

commit v7 on v6

--- a/solution.py
+++ b/solution.py
@@ -122,14 +122,19 @@
     def cols(h):
         return pl.ds(h * half, half)
 
-    fine = half // U
-    G = H * U
+    cut = [(0, u * (half // U), half // U) for u in range(U)] + [(h, 0, half) for h in range(1, H)]
+    G = len(cut)
 
     def fine_cols(g):
-        return pl.ds(g * fine, fine)
+        h, at, size = cut[g]
+        return pl.ds(h * half + at, size)
 
     def rows_of(g, dev):
-        return lbuf.at[g // U, dev, :, pl.ds(g % U * fine, fine)]
+        h, at, size = cut[g]
+        return lbuf.at[h, dev, :, pl.ds(at, size)]
+
+    def parts_of(h):
+        return [g for g in range(G) if cut[g][0] == h]
 
     def late_copy(g):
         return remote(
@@ -208,7 +213,7 @@
 
     def lend(way, k, h, lane):
         piece = rows_of(h, source(way, k) * 2 + lane)
-        return remote(piece, piece, agp_s, agp_r.at[h // U], s, partner)
+        return remote(piece, piece, agp_s, agp_r.at[cut[h][0]], s, partner)
 
     def own(h):
         @pl.when(s == 0)
@@ -381,7 +386,7 @@
         for g in range(G):
             relay(k, g)
     for h in range(H):
-        for g in range(h * U, h * U + U):
+        for g in parts_of(h):
             relay(last, g)
         if h == H - 1:
             grad_wait(steps)
@@ -391,6 +396,7 @@
             gathered(h - 1)
             activate(h - 1)
             expand(h - 1)
+
     gathered(H - 1)
     activate(H - 1)
     expand(H - 1)
@@ -402,22 +408,39 @@
     def pair_copy(h):
         return remote(part.at[other, h], prx.at[h], px_s, px_r.at[h], s, partner)
 
+    rem = rows % 8
+    main = rows - rem
+    tall = part.shape[3]
+
+    height = (pl.ds(0, main), pl.ds(0, tall))
+
+    def forms(h, body):
+        @pl.when(h < H - 1)
+        def _():
+            body(0)
+
+        @pl.when(h == H - 1)
+        def _():
+            body(1)
+
     def mine(h, chip):
         return part[c, h, chip].astype(F32) + prx[h, chip].astype(F32)
 
     def goal(way, m):
         return last - m if way == 0 else m
 
-    def row_hop(way, r):
+    def row_hop(way, r, kind):
         m, h = r // H, lax.rem(r, H)
-        to = goal(way, m)
-        return remote(part.at[c, h, to], rx.at[way, h, to], row_s.at[way], row_r.at[way, r], s, nxt[way])
+        to, at = goal(way, m), height[kind]
+        return remote(
+            part.at[c, h, to, at], rx.at[way, h, to, at], row_s.at[way, kind], row_r.at[way, r], s, nxt[way],
+        )
 
     def row_start(way, r):
         m, h = r // H, lax.rem(r, H)
         to = goal(way, m)
         part[c, h, to] = mine(h, to).astype(BF16)
-        row_hop(way, r).start()
+        forms(h, lambda kind: row_hop(way, r, kind).start())
 
     def row_relay(way, r):
         m, h = r // H, lax.rem(r, H)
@@ -425,9 +448,9 @@
 
         @pl.when(last - m > hops[way])
         def _():
-            row_hop(way, r).wait_recv()
+            forms(h, lambda kind: row_hop(way, r, kind).wait_recv())
             part[c, h, to] = (mine(h, to) + rx[way, h, to].astype(F32)).astype(BF16)
-            row_hop(way, r).start()
+            forms(h, lambda kind: row_hop(way, r, kind).start())
 
     def scatter(h):
         pair_copy(h).wait_recv()
@@ -441,7 +464,11 @@
         for n in range(half // tile):
             value = dot(hidden[...], wred[:, pl.ds(h * half + n * tile, tile)]).astype(BF16)
             for dev in range(n_dev):
-                part[dev % 2, h, dev // 2, :, pl.ds(n * tile, tile)] = value[dev * padded:dev * padded + rows]
+                low, col = dev * padded, pl.ds(n * tile, tile)
+                part[dev % 2, h, dev // 2, 0:main, col] = value[low:low + main]
+                if rem:
+                    tail = main + rem * h
+                    part[dev % 2, H - 1, dev // 2, tail:tail + rem, col] = value[low + main:low + rows]
         pair_copy(h).start()
         if h < steps:
             grad_wait(h)
@@ -504,7 +531,6 @@
     each(lead, far, rest)
     count = far + share
     farther = jnp.maximum(hops[0], hops[1])
-    calm = H + 2 * SKEW
 
     def slot(t):
         for way in range(2):
@@ -536,10 +562,6 @@
         @pl.when(both(i >= 0, i < share))
         def _():
             sum_finish(i)
-
-        @pl.when(both(t >= calm, t < calm + steps))
-        def _():
-            downward(t - calm)
 
     @pl.when(s < sections - 1)
     def _():
@@ -558,21 +580,36 @@
         def _():
             span(gtx.at[0:mass], gx_s, gx_r.at[0]).wait_send()
 
-    each(SKEW, max(H + share + SKEW * last, calm + steps), slot)
+    @pl.when(farther == last)
+    def _():
+        each(0, steps, downward)
+
+    each(SKEW, H + share + SKEW * last, slot)
+
+    @pl.when(farther < last)
+    def _():
+        each(0, steps, downward)
+
 
     for h in range(H):
         for way in range(2):
             @pl.when(hops[way] > 0)
             def _():
-                row_hop(way, (last - hops[way]) * H + h).wait_recv()
+                row_hop(way, (last - hops[way]) * H + h, h // (H - 1)).wait_recv()
         value = mine(h, q) + rx[0, h, q].astype(F32) + rx[1, h, q].astype(F32)
-        late_out[:, cols(h)] = (lbuf[h, d].astype(F32) + value).astype(BF16)
+        late_out[0:main, cols(h)] = (lbuf[h, d, 0:main].astype(F32) + value[0:main]).astype(BF16)
+    if rem:
+        for h in range(H):
+            tail = main + rem * h
+            end = lbuf[h, d, main:rows].astype(F32) + value[tail:tail + rem]
+            late_out[main:rows, cols(h)] = end.astype(BF16)
 
     for way in range(2):
         for k in range(last):
             @pl.when(hops[way] == k)
             def _():
-                span(prx.at[:, 0:last - k], row_s.at[way], px_r.at[0]).wait_send()
+                for kind, planes in enumerate((pl.ds(0, H - 1), pl.ds(H - 1, 1))):
+                    span(prx.at[planes, 0:last - k, height[kind]], row_s.at[way, kind], px_r.at[0]).wait_send()
     for lane in range(2):
         mass = share + front * lane
         block = gout.at[lane * share:lane * share + mass]
@@ -611,9 +648,9 @@
         send(wide_e.at[at], gexp.at[0, at])
     for n in range(fe // 256):
         at = pl.ds(n * 256, 256)
-        wide_r[at, 0:front * depth] = sums[2 * share:, :, at].reshape(front * depth, 256).astype(F32).T
+        wide_r[at, 0:front * depth] = sums[2 * share:, :, at].reshape(front * depth, 256).T.astype(F32)
         later = [sums[lane:lane + half_r, :, at].reshape(half_r * depth, 256) for lane in (0, share)]
-        wide_r[at, front * depth:] = jnp.concatenate(later).astype(F32).T
+        wide_r[at, front * depth:] = jnp.concatenate(later).T.astype(F32)
         send(wide_r.at[at], gred.at[0, at])
     for copy in copies:
         copy.wait()
@@ -631,6 +668,7 @@
     Q = n_dev // 2
     half = cl // H
     padded = -(-rows // 16) * 16
+    tall = rows + (H - 1) * (rows % 8)
     chunk = max(k for k in range(16, 257, 16) if e_rows % k == 0)
     steps = e_rows // chunk
     pieces, front, share = cuts(ce)
@@ -657,9 +695,9 @@
             V((n_dev * padded, cl), BF16),
             V((n_dev * padded, hid) if split else (8, 128), F32),
             V((n_dev * padded, hid), BF16),
-            V((2, H, Q, rows, half), BF16),
-            V((H, Q, rows, half), BF16),
-            V((2, H, Q, rows, half), BF16),
+            V((2, H, Q, tall, half), BF16),
+            V((H, Q, tall, half), BF16),
+            V((2, H, Q, tall, half), BF16),
             V((cl, hid), BF16),
             V((hid, cl), BF16),
             V((e_rows, ce), BF16),
@@ -678,9 +716,9 @@
             V((1, cl), F32),
             V((1, hid), F32),
             V((1, hid), F32),
-            dma((10,)), dma((H * U,)), dma((steps + 1,)), dma((2, Q - 1, H * U)), dma((H,)), dma((H,)),
+            dma((10,)), dma((H + U - 1,)), dma((steps + 1,)), dma((2, Q - 1, H + U - 1)), dma((H,)), dma((H,)),
             dma((4,)), dma((2, (Q - 1) * H)), dma((2, own)), dma,
-            dma, dma, dma((2,)), dma, dma, dma, dma((2,)), dma((2,)), dma,
+            dma, dma, dma((2,)), dma, dma, dma, dma((2, 2)), dma((2,)), dma,
         ],
         compiler_params=pltpu.CompilerParams(
             collective_id=0, has_side_effects=True, vmem_limit_bytes=60 * 1024 * 1024

time: 55.6 us -> 55 us (0.989)
  no operation moved by 1% of the time
where the time goes in v7:
time: 55 us; the launch traced here: 54.6 us
  Pallas kernels  54 us (98%)
  between operations  0.64 us (1%)
    pallas_call x1, Pallas kernels, shards(): pl.pallas_call(functools.partial(kernel, sections, n_dev, chunk, split),...  52.3 us
    pallas_call x1, Pallas kernels, shards(): pl.pallas_call(finish, out_shape=(jax.ShapeDtypeStruct((1, rows, cl), BF1...  1.71 us

profile of v7, /device:TPU:5, one launch (start us, length us, event | category | flops | bytes accessed | tf_op | source)
XLA Modules:
  0.0 54.6 jit_solution(3696197734417349523)
XLA Ops:
  0.6 52.3 %relay.1 = (bf16[98,1024]{1,0:T(8,128)(2,1)S(1)}, bf16[1568,256]{1,0:T(8,128)(2,1)S(1)}, bf16[32,16,1024]{2,1,0:T(8,128)(2,1)S(1)}) custom-call(bf16[98,1024]{1,0:T(8,128)(2,1)} %bitcast.13, bf16[98,1024]{1,0:T(8,128)(2,1)} %entry_hbm.1, f32[1,1024]{1,0:T(1,128)} %gain1_hbm.1, f32[1,1024]{1,0:T(1,128)} %shift1_hbm.1, bf16[1024,512]{1,0:T(8,128)(2,1)} %bitcast.7, ...), custom_call_target="tpu_custom_call" | custom-call | tf_op jit(solution)/shard_map/relay/pallas_call | solution.py:683
  52.9 1.7 %finish.1 = (bf16[1,98,1024]{2,1,0:T(8,128)(2,1)}, bf16[1,1568,256]{2,1,0:T(8,128)(2,1)}, f32[1,256,1024]{2,1,0:T(8,128)}, f32[1,1024,256]{2,1,0:T(8,128)}) custom-call(bf16[98,1024]{1,0:T(8,128)(2,1)S(1)} %get-tuple-element.7.late_in, bf16[1568,256]{1,0:T(8,128)(2,1)S(1)} %get-tuple-element.8.grad_in, bf16[32,16,1024]{2,1,0:T(8,128)(2,1)S(1)} %get-tuple-element.9.sums), custom_call_target="tpu_custom_call" | custom-call | tf_op jit(solution)/shard_map/finish/pallas_call | solution.py:731

commit v8 on v7

--- a/solution.py
+++ b/solution.py
@@ -13,7 +13,7 @@
 H = 4
 U = 2
 SKEW = 4
-LEAD = 0
+LEAD = 1
 F32 = jnp.float32
 BF16 = jnp.bfloat16
 

time: 55 us -> 54.9 us (level)
  no operation moved by 1% of the time
where the time goes in v8:
time: 54.9 us; the launch traced here: 54.5 us
  Pallas kernels  53.9 us (98%)
  between operations  0.64 us (1%)
    pallas_call x1, Pallas kernels, shards(): pl.pallas_call(functools.partial(kernel, sections, n_dev, chunk, split),...  52.2 us
    pallas_call x1, Pallas kernels, shards(): pl.pallas_call(finish, out_shape=(jax.ShapeDtypeStruct((1, rows, cl), BF1...  1.71 us

profile of v8, /device:TPU:5, one launch (start us, length us, event | category | flops | bytes accessed | tf_op | source)
XLA Modules:
  0.0 54.5 jit_solution(3948899930355734633)
XLA Ops:
  0.6 52.2 %relay.1 = (bf16[98,1024]{1,0:T(8,128)(2,1)S(1)}, bf16[1568,256]{1,0:T(8,128)(2,1)S(1)}, bf16[32,16,1024]{2,1,0:T(8,128)(2,1)S(1)}) custom-call(bf16[98,1024]{1,0:T(8,128)(2,1)} %bitcast.13, bf16[98,1024]{1,0:T(8,128)(2,1)} %entry_hbm.1, f32[1,1024]{1,0:T(1,128)} %gain1_hbm.1, f32[1,1024]{1,0:T(1,128)} %shift1_hbm.1, bf16[1024,512]{1,0:T(8,128)(2,1)} %bitcast.7, ...), custom_call_target="tpu_custom_call" | custom-call | tf_op jit(solution)/shard_map/relay/pallas_call | solution.py:683
  52.8 1.7 %finish.1 = (bf16[1,98,1024]{2,1,0:T(8,128)(2,1)}, bf16[1,1568,256]{2,1,0:T(8,128)(2,1)}, f32[1,256,1024]{2,1,0:T(8,128)}, f32[1,1024,256]{2,1,0:T(8,128)}) custom-call(bf16[98,1024]{1,0:T(8,128)(2,1)S(1)} %get-tuple-element.7.late_in, bf16[1568,256]{1,0:T(8,128)(2,1)S(1)} %get-tuple-element.8.grad_in, bf16[32,16,1024]{2,1,0:T(8,128)(2,1)S(1)} %get-tuple-element.9.sums), custom_call_target="tpu_custom_call" | custom-call | tf_op jit(solution)/shard_map/finish/pallas_call | solution.py:731
